TPU v7x, 32 devices: a whole 2x2x4 slice. The times are simulated.
32 devices in a mesh: gx: 4 (over y, x), gy: 8 (over z, core).
Axes of the slice: x: 2, y: 2, z: 4, core: 2. Of those that a mesh axis runs over, the one named last changes fastest.
Arguments:
- embeddings: bfloat16 [163840, 1024], P(('gx', 'gy')), may hold values from -6 to 6
- device_local_selections: int32 [32, 64], P(('gx', 'gy')), may hold values from 0 to 5119
- merge_picks: int32 [32, 64], replicated, may hold values from 0 to 127
Outputs:
- final_centers: bfloat16 [64, 1024], replicated
- coverage: float32 [163840], P(('gx', 'gy'))
- radius: float32 [], replicated
All inputs are finite; a program needn't handle non-finite values.
Results may differ from a plain program's by a relative error of at most 0.001.
Values may be sent and summed in bfloat16 or wider, within the bound.
No kernel may reach another device: no remote copies, remote signals or barrier semaphores. Data moves between devices by JAX's collectives and lax.ppermute only.
A program may use at most 64 MiB of HBM per device.

v0:
```python
import jax
import jax.numpy as jnp
from jax import lax
from jax.sharding import PartitionSpec as P


def swapped(value, axis, distance):
    mask = 2**distance
    pairs = [(source, source ^ mask) for source in range(lax.axis_size(axis))]
    return lax.ppermute(value, axis, pairs)


def nearest(points, squares, chosen_centroids, width):
    wide = chosen_centroids.astype(jnp.float32)
    csq = jnp.sum(wide * wide, axis=1)
    prod = jnp.dot(points, chosen_centroids.T, preferred_element_type=jnp.float32)
    return jnp.min(squares[:, None] - 2.0 * prod + csq[None, :], axis=1) / width


def choose_again(combined_selection, selected_indices, center_count):
    onehot = (
        lax.broadcasted_iota(jnp.int32, (selected_indices.shape[0], center_count), 1)
        == selected_indices[:, None]
    ).astype(jnp.bfloat16)
    return jnp.dot(onehot, combined_selection, preferred_element_type=jnp.float32).astype(
        jnp.bfloat16
    )


def per_device(embeddings, device_local_selections, merge_picks):
    rows, width = embeddings.shape
    chosen_centroids = device_local_selections.shape[1]
    size_gx = lax.axis_size("gx")
    size_gy = lax.axis_size("gy")
    devices = size_gx * size_gy
    index_gx = lax.axis_index("gx")
    index_gy = lax.axis_index("gy")
    mine = index_gx * size_gy + index_gy
    onehot = (
        lax.broadcasted_iota(jnp.int32, (chosen_centroids, rows), 1)
        == device_local_selections[0][:, None]
    ).astype(jnp.bfloat16)
    sets = jnp.dot(onehot, embeddings, preferred_element_type=jnp.float32).astype(jnp.bfloat16)
    wide = embeddings.astype(jnp.float32)
    squares = jnp.sum(wide * wide, axis=1)
    seen = [sets]
    cover = nearest(embeddings, squares, sets, width)

    def account(cover, other):
        seen.append(other)
        return cover

    def combine(sets, other, step, number):
        lower = number >> step & 1 == 0
        combined_selection = jnp.where(
            lower, jnp.concatenate([sets, other], 0), jnp.concatenate([other, sets], 0)
        )
        row = devices - (devices >> step) + (number >> step + 1)
        selected_indices = lax.dynamic_index_in_dim(merge_picks, row, 0, keepdims=False)
        return choose_again(combined_selection, selected_indices, 2 * chosen_centroids)

    bits_gy = size_gy.bit_length() - 1
    horizontal_grid_bits = size_gx.bit_length() - 1
    for step in range(bits_gy):
        other = swapped(sets, "gy", step)
        cover = account(cover, other)
        sets = combine(sets, other, step, mine)
    for level in range(horizontal_grid_bits):
        step = bits_gy + level
        other = swapped(sets, "gx", level)
        cover = account(cover, other)
        sets = combine(sets, other, step, mine)
    cover = nearest(embeddings, squares, jnp.concatenate(seen, axis=0), width)
    radius = lax.pmax(jnp.max(cover), ("gx", "gy"))
    return (sets, cover, radius)


def solution(mesh):
    return jax.shard_map(
        per_device,
        mesh=mesh,
        in_specs=(P(("gx", "gy"), None), P(("gx", "gy"), None), P()),
        out_specs=(P(), P(("gx", "gy")), P()),
        check_vma=False,
    )
```

profile of v0, /device:TPU:0, one launch (start us, length us, event | category | flops | bytes accessed | tf_op | source)
XLA Modules:
  0.0 89.0 jit_solution(1292984045285618340)
XLA Ops:
  0.6 6.0 %constant_dynamic-update-slice_fusion.5 = (bf16[384,1024]{1,0:T(8,128)(2,1)S(1)}, bf16[64,1024]{1,0:T(8,128)(2,1)S(1)}) fusion(bf16[5120,1024]{1,0:T(8,128)(2,1)} %param.3, s32[64]{0:T(128)} %bitcast.14), kind=kOutput, calls=%fused_computation.62 | convolution fusion | flops 671481856 | bytes 10748160 | tf_op jit(solution)/shard_map/dot_general | solution.py:43
  6.6 0.6 collective-permute-start
  7.2 0.8 fusion.38
  8.0 0.2 collective-permute-done
  8.2 0.2 convolution_convert_fusion.4
  8.4 3.0 %collective-permute-start.1 = (bf16[64,1024]{1,0:T(8,128)(2,1)S(1)}, bf16[64,1024]{1,0:T(8,128)(2,1)S(1)}, u32[]{:S(2)}, u32[]{:S(2)}) collective-permute-start(bf16[64,1024]{1,0:T(8,128)(2,1)S(1)} %convolution_convert_fusion.4), channel_id=1, source_target_pairs={{0,2},{1,3},{2,0},{3,1},{4,6},{5,7},{6,4},{7,5},{8,10},{9,11},{10,... | collective-permute-start | bytes 393224 | tf_op jit(solution)/shard_map/ppermute | solution.py:10
  11.4 3.8 %collective-permute-done.1 = bf16[64,1024]{1,0:T(8,128)(2,1)S(1)} collective-permute-done((bf16[64,1024]{1,0:T(8,128)(2,1)S(1)}, bf16[64,1024]{1,0:T(8,128)(2,1)S(1)}, u32[]{:S(2)}, u32[]{:S(2)}) %collective-permute-start.1) | collective-permute-done | bytes 131104 | tf_op jit(solution)/shard_map/ppermute | solution.py:10
  15.2 0.2 convolution_convert_fusion.3
  15.4 2.8 %collective-permute-start.2 = (bf16[64,1024]{1,0:T(8,128)(2,1)S(1)}, bf16[64,1024]{1,0:T(8,128)(2,1)S(1)}, u32[]{:S(2)}, u32[]{:S(2)}) collective-permute-start(bf16[64,1024]{1,0:T(8,128)(2,1)S(1)} %convolution_convert_fusion.3), channel_id=1, source_target_pairs={{0,4},{1,5},{2,6},{3,7},{4,0},{5,1},{6,2},{7,3},{8,12},{9,13},{10,... | collective-permute-start | bytes 393224 | tf_op jit(solution)/shard_map/ppermute | solution.py:10
  18.2 6.1 %multiply_reduce_fusion = f32[5120]{0:T(1024)S(1)} fusion(bf16[5120,1024]{1,0:T(8,128)(2,1)} %param.3), kind=kLoop, calls=%fused_computation | loop fusion | flops 15723520 | bytes 10506240 | tf_op jit(solution)/shard_map/reduce_sum | solution.py:45
  24.3 0.0 collective-permute-done.2
  24.4 0.2 convolution_convert_fusion.2
  24.6 1.6 %collective-permute-start.3 = (bf16[64,1024]{1,0:T(8,128)(2,1)S(1)}, bf16[64,1024]{1,0:T(8,128)(2,1)S(1)}, u32[]{:S(2)}, u32[]{:S(2)}) collective-permute-start(bf16[64,1024]{1,0:T(8,128)(2,1)S(1)} %convolution_convert_fusion.2), channel_id=1, source_target_pairs={{0,8},{8,0},{16,24},{24,16},{1,9},{9,1},{17,25},{25,17},{2,10},{10... | collective-permute-start | bytes 393224 | tf_op jit(solution)/shard_map/ppermute | solution.py:10
  26.2 3.4 %collective-permute-done.3 = bf16[64,1024]{1,0:T(8,128)(2,1)S(1)} collective-permute-done((bf16[64,1024]{1,0:T(8,128)(2,1)S(1)}, bf16[64,1024]{1,0:T(8,128)(2,1)S(1)}, u32[]{:S(2)}, u32[]{:S(2)}) %collective-permute-start.3) | collective-permute-done | bytes 131104 | tf_op jit(solution)/shard_map/ppermute | solution.py:10
  29.6 0.2 convolution_convert_fusion.1
  29.9 1.6 %collective-permute-start.4 = (bf16[64,1024]{1,0:T(8,128)(2,1)S(1)}, bf16[64,1024]{1,0:T(8,128)(2,1)S(1)}, u32[]{:S(2)}, u32[]{:S(2)}) collective-permute-start(bf16[64,1024]{1,0:T(8,128)(2,1)S(1)} %convolution_convert_fusion.1), channel_id=1, source_target_pairs={{0,16},{8,24},{16,0},{24,8},{1,17},{9,25},{17,1},{25,9},{2,18},{10... | collective-permute-start | bytes 393224 | tf_op jit(solution)/shard_map/ppermute | solution.py:10
  31.5 3.4 %collective-permute-done.4 = bf16[64,1024]{1,0:T(8,128)(2,1)S(1)} collective-permute-done((bf16[64,1024]{1,0:T(8,128)(2,1)S(1)}, bf16[64,1024]{1,0:T(8,128)(2,1)S(1)}, u32[]{:S(2)}, u32[]{:S(2)}) %collective-permute-start.4) | collective-permute-done | bytes 131104 | tf_op jit(solution)/shard_map/ppermute | solution.py:10
  34.9 0.2 multiply_reduce_fusion.1
  35.1 11.3 %add_reduce_fusion = f32[5120]{0:T(1024)S(1)} fusion(f32[384]{0:T(512)S(1)} %multiply_reduce_fusion.1, f32[5120]{0:T(1024)S(1)} %multiply_reduce_fusion, bf16[384,1024]{1,0:T(8,128)(2,1)S(1)} %constant_dynamic-update-slice_fusion, bf16[5120,1024]{1,0:T(8,128)(2,1)} %param.3), kind=kOutput, calls=%fused_computation.1 | convolution fusion | flops 4034391040 | bytes 11314688 | tf_op jit(solution)/shard_map/dot_general | solution.py:16
  46.5 1.2 %fusion.48 = (f32[]{:T(128)}, f32[5120]{0:T(1024)}) fusion(f32[5120]{0:T(1024)S(1)} %add_reduce_fusion), kind=kLoop, calls=%fused_computation.79 | loop fusion | flops 10239 | bytes 40964 | tf_op jit(solution)/shard_map/reduce_max | solution.py:74
  47.7 40.4 %pmax.7 = f32[]{:T(128)} all-reduce(f32[]{:T(128)} %get-tuple-element.3), channel_id=1, replica_groups=mesh['gx'=4,'gy'=8] {'gx','gy'}, use_global_device_ids=true, to_apply=%region_4.5 | all-reduce | flops 1 | bytes 8 | tf_op jit(solution)/shard_map/pmax | solution.py:74
  88.1 0.9 %convolution_convert_fusion = bf16[64,1024]{1,0:T(8,128)(2,1)} fusion(bf16[64,1024]{1,0:T(8,128)(2,1)S(1)} %collective-permute-done.4, bf16[64,1024]{1,0:T(8,128)(2,1)S(1)} %convolution_convert_fusion.1, pred[]{:T(512)S(6)} %eq.78, s32[64]{0:T(128)S(1)} %get-tuple-element.5), kind=kOutput, calls=%fused_computation.5 | convolution fusion | flops 18030592 | bytes 393473 | tf_op jit(solution)/shard_map/dot_general | solution.py:25
  (5 shorter events, 0.1 us)
Async XLA Ops:
  6.6 1.5 %collective-permute-start = (bf16[64,1024]{1,0:T(8,128)(2,1)S(1)}, bf16[64,1024]{1,0:T(8,128)(2,1)S(1)}, u32[]{:S(2)}, u32[]{:S(2)}) collective-permute-start(bf16[64,1024]{1,0:T(8,128)(2,1)S(1)} %get-tuple-element.11), channel_id=1, source_target_pairs={{0,1},{1,0},{2,3},{3,2},{4,5},{5,4},{6,7},{7,6},{8,9},{9,8},{10,11... | collective-permute-start | bytes 393224 | tf_op jit(solution)/shard_map/ppermute | solution.py:10
  8.4 6.8 %collective-permute-start.1 = (bf16[64,1024]{1,0:T(8,128)(2,1)S(1)}, bf16[64,1024]{1,0:T(8,128)(2,1)S(1)}, u32[]{:S(2)}, u32[]{:S(2)}) collective-permute-start(bf16[64,1024]{1,0:T(8,128)(2,1)S(1)} %convolution_convert_fusion.4), channel_id=1, source_target_pairs={{0,2},{1,3},{2,0},{3,1},{4,6},{5,7},{6,4},{7,5},{8,10},{9,11},{10,... | collective-permute-start | bytes 393224 | tf_op jit(solution)/shard_map/ppermute | solution.py:10
  15.4 8.9 %collective-permute-start.2 = (bf16[64,1024]{1,0:T(8,128)(2,1)S(1)}, bf16[64,1024]{1,0:T(8,128)(2,1)S(1)}, u32[]{:S(2)}, u32[]{:S(2)}) collective-permute-start(bf16[64,1024]{1,0:T(8,128)(2,1)S(1)} %convolution_convert_fusion.3), channel_id=1, source_target_pairs={{0,4},{1,5},{2,6},{3,7},{4,0},{5,1},{6,2},{7,3},{8,12},{9,13},{10,... | collective-permute-start | bytes 393224 | tf_op jit(solution)/shard_map/ppermute | solution.py:10
  24.6 5.0 %collective-permute-start.3 = (bf16[64,1024]{1,0:T(8,128)(2,1)S(1)}, bf16[64,1024]{1,0:T(8,128)(2,1)S(1)}, u32[]{:S(2)}, u32[]{:S(2)}) collective-permute-start(bf16[64,1024]{1,0:T(8,128)(2,1)S(1)} %convolution_convert_fusion.2), channel_id=1, source_target_pairs={{0,8},{8,0},{16,24},{24,16},{1,9},{9,1},{17,25},{25,17},{2,10},{10... | collective-permute-start | bytes 393224 | tf_op jit(solution)/shard_map/ppermute | solution.py:10
  29.9 5.0 %collective-permute-start.4 = (bf16[64,1024]{1,0:T(8,128)(2,1)S(1)}, bf16[64,1024]{1,0:T(8,128)(2,1)S(1)}, u32[]{:S(2)}, u32[]{:S(2)}) collective-permute-start(bf16[64,1024]{1,0:T(8,128)(2,1)S(1)} %convolution_convert_fusion.1), channel_id=1, source_target_pairs={{0,16},{8,24},{16,0},{24,8},{1,17},{9,25},{17,1},{25,9},{2,18},{10... | collective-permute-start | bytes 393224 | tf_op jit(solution)/shard_map/ppermute | solution.py:10
where the time goes:
time: 89.3 us; the launch traced here: 89 us
  blocking collectives  40.4 us (45%)
  matrix products  19.1 us (21%)
  waiting for transfers between devices  10.9 us (12%)
  starting transfers between devices  9.5 us (11%)
  other arithmetic  7.54 us (8%)
    pmax x1, blocking collectives, per_device(): radius = lax.pmax(jnp.max(cover), ('gx', 'gy'))  40.4 us
    dot_general x1, matrix products, nearest(): jnp.dot(points, chosen_centroids.T, preferred_element_type=jnp.float32)  11.3 us
    ppermute x5, waiting for transfers between devices, swapped(): return lax.ppermute(value, axis, pairs)  10.9 us
    ppermute x5, starting transfers between devices, swapped(): return lax.ppermute(value, axis, pairs)  9.5 us
    reduce_sum x1, other arithmetic, per_device(): squares = jnp.sum(wide * wide, axis=1)  6.09 us
    dot_general x1, matrix products, per_device(): jnp.dot(onehot, embeddings, preferred_element_type=jnp.float32)  5.98 us
  transfers between devices with their start and end apart: 5, of which 4 were waited for; matrix products, arithmetic and copies ran while one was open for 8% of the time, Pallas kernels for 0%

commit v1 on v0

--- a/solution.py
+++ b/solution.py
@@ -71,8 +71,14 @@
         cover = account(cover, other)
         sets = combine(sets, other, step, mine)
     cover = nearest(embeddings, squares, jnp.concatenate(seen, axis=0), width)
-    radius = lax.pmax(jnp.max(cover), ("gx", "gy"))
-    return (sets, cover, radius)
+    peak = jnp.broadcast_to(jnp.max(cover), (8, 128))
+    bit = 1
+    while bit < devices:
+        mask = bit | 1
+        pairs = [(source, source ^ mask) for source in range(devices)]
+        peak = jnp.maximum(peak, lax.ppermute(peak, ("gx", "gy"), pairs))
+        bit *= 2
+    return (sets, cover, peak[0, 0])
 
 
 def solution(mesh):

time: 89.3 us -> 64.9 us (0.73)
  blocking collectives: 40.4 us -> 0 us
  waiting for transfers between devices: 10.9 us -> 18.2 us
  starting transfers between devices: 9.5 us -> 15.6 us
  other arithmetic: 7.54 us -> 8.84 us
  local copies, waits for them, and re-layouts: 0.86 us -> 2.02 us
    pmax x1 -> x0, blocking collectives: 40.4 us -> none  [per_device(): radius = lax.pmax(jnp.max(cover), ('gx', 'gy'))]
    ppermute x0 -> x5, waiting for transfers between devices: none -> 7.39 us  [per_device(): peak = jnp.maximum(peak, lax.ppermute(peak, ('gx', 'gy'), pairs))]
    ppermute x0 -> x5, starting transfers between devices: none -> 6.1 us  [per_device(): peak = jnp.maximum(peak, lax.ppermute(peak, ('gx', 'gy'), pairs))]
    max x0 -> x5, other arithmetic: none -> 1.31 us  [per_device(): peak = jnp.maximum(peak, lax.ppermute(peak, ('gx', 'gy'), pairs))]
  transfers between devices with their start and end apart: 5 -> 10, of which waited for: 4 -> 9; matrix products, arithmetic and copies ran while one was open for 8% -> 12% of each run, Pallas kernels for 0% -> 0%
where the time goes in v1:
time: 64.9 us; the launch traced here: 64.6 us
  matrix products  19.1 us (29%)
  waiting for transfers between devices  18.2 us (28%)
  starting transfers between devices  15.6 us (24%)
  other arithmetic  8.84 us (14%)
  local copies, waits for them, and re-layouts  2.02 us (3%)
  between operations  0.77 us (1%)
    dot_general x1, matrix products, nearest(): jnp.dot(points, chosen_centroids.T, preferred_element_type=jnp.float32)  11.3 us
    ppermute x5, waiting for transfers between devices, swapped(): return lax.ppermute(value, axis, pairs)  10.9 us
    ppermute x5, starting transfers between devices, swapped(): return lax.ppermute(value, axis, pairs)  9.5 us
    ppermute x5, waiting for transfers between devices, per_device(): peak = jnp.maximum(peak, lax.ppermute(peak, ('gx', 'gy'), pairs))  7.39 us
    ppermute x5, starting transfers between devices, per_device(): peak = jnp.maximum(peak, lax.ppermute(peak, ('gx', 'gy'), pairs))  6.1 us
    reduce_sum x1, other arithmetic, per_device(): squares = jnp.sum(wide * wide, axis=1)  6.09 us
    dot_general x1, matrix products, per_device(): jnp.dot(onehot, embeddings, preferred_element_type=jnp.float32)  5.98 us
    dot_general x5, matrix products, choose_again(): jnp.dot(onehot, combined_selection, preferred_element_type=jnp.float32)  1.78 us
  transfers between devices with their start and end apart: 10, of which 9 were waited for; matrix products, arithmetic and copies ran while one was open for 12% of the time, Pallas kernels for 0%

profile of v1, /device:TPU:0, one launch (start us, length us, event | category | flops | bytes accessed | tf_op | source)
XLA Modules:
  0.0 64.6 jit_solution(12373495811354386898)
XLA Ops:
  0.6 6.0 %constant_dynamic-update-slice_fusion.5 = (bf16[384,1024]{1,0:T(8,128)(2,1)S(1)}, bf16[64,1024]{1,0:T(8,128)(2,1)S(1)}) fusion(bf16[5120,1024]{1,0:T(8,128)(2,1)} %param.3, s32[64]{0:T(128)} %bitcast.15), kind=kOutput, calls=%fused_computation.62 | convolution fusion | flops 671481856 | bytes 10748160 | tf_op jit(solution)/shard_map/dot_general | solution.py:43
  6.6 0.6 collective-permute-start
  7.2 0.8 %fusion.38 = (s32[64]{0:T(128)S(1)}, s32[64]{0:T(128)S(1)}, s32[64]{0:T(128)S(1)}, s32[64]{0:T(128)S(1)}, s32[64]{0:T(128)S(1)}) fusion(s32[32,64]{1,0:T(8,128)} %param.5, s32[]{:T(128)S(6)} %select_n.48, s32[]{:T(128)S(6)} %select_n.52, s32[]{:T(128)S(6)} %select_n.50, s32[]{:T(128)S(6)} %select_n.56, s32[]{:T(128)S(6)} %select_n.54), kind=kLoop, calls=%fused_computation.70 | loop fusion | bytes 2580 | tf_op jit(solution)/shard_map/eq | solution.py:22
  8.0 0.2 collective-permute-done
  8.2 0.2 convolution_convert_fusion.4
  8.4 3.0 %collective-permute-start.1 = (bf16[64,1024]{1,0:T(8,128)(2,1)S(1)}, bf16[64,1024]{1,0:T(8,128)(2,1)S(1)}, u32[]{:S(2)}, u32[]{:S(2)}) collective-permute-start(bf16[64,1024]{1,0:T(8,128)(2,1)S(1)} %convolution_convert_fusion.4), channel_id=1, source_target_pairs={{0,2},{1,3},{2,0},{3,1},{4,6},{5,7},{6,4},{7,5},{8,10},{9,11},{10,... | collective-permute-start | bytes 393224 | tf_op jit(solution)/shard_map/ppermute | solution.py:10
  11.4 3.8 %collective-permute-done.1 = bf16[64,1024]{1,0:T(8,128)(2,1)S(1)} collective-permute-done((bf16[64,1024]{1,0:T(8,128)(2,1)S(1)}, bf16[64,1024]{1,0:T(8,128)(2,1)S(1)}, u32[]{:S(2)}, u32[]{:S(2)}) %collective-permute-start.1) | collective-permute-done | bytes 131104 | tf_op jit(solution)/shard_map/ppermute | solution.py:10
  15.2 0.2 convolution_convert_fusion.3
  15.4 2.8 %collective-permute-start.2 = (bf16[64,1024]{1,0:T(8,128)(2,1)S(1)}, bf16[64,1024]{1,0:T(8,128)(2,1)S(1)}, u32[]{:S(2)}, u32[]{:S(2)}) collective-permute-start(bf16[64,1024]{1,0:T(8,128)(2,1)S(1)} %convolution_convert_fusion.3), channel_id=1, source_target_pairs={{0,4},{1,5},{2,6},{3,7},{4,0},{5,1},{6,2},{7,3},{8,12},{9,13},{10,... | collective-permute-start | bytes 393224 | tf_op jit(solution)/shard_map/ppermute | solution.py:10
  18.2 6.1 %multiply_reduce_fusion = f32[5120]{0:T(1024)S(1)} fusion(bf16[5120,1024]{1,0:T(8,128)(2,1)} %param.3), kind=kLoop, calls=%fused_computation | loop fusion | flops 15723520 | bytes 10506240 | tf_op jit(solution)/shard_map/reduce_sum | solution.py:45
  24.3 0.0 collective-permute-done.2
  24.4 0.2 convolution_convert_fusion.2
  24.6 1.6 %collective-permute-start.3 = (bf16[64,1024]{1,0:T(8,128)(2,1)S(1)}, bf16[64,1024]{1,0:T(8,128)(2,1)S(1)}, u32[]{:S(2)}, u32[]{:S(2)}) collective-permute-start(bf16[64,1024]{1,0:T(8,128)(2,1)S(1)} %convolution_convert_fusion.2), channel_id=1, source_target_pairs={{0,8},{8,0},{16,24},{24,16},{1,9},{9,1},{17,25},{25,17},{2,10},{10... | collective-permute-start | bytes 393224 | tf_op jit(solution)/shard_map/ppermute | solution.py:10
  26.2 3.4 %collective-permute-done.3 = bf16[64,1024]{1,0:T(8,128)(2,1)S(1)} collective-permute-done((bf16[64,1024]{1,0:T(8,128)(2,1)S(1)}, bf16[64,1024]{1,0:T(8,128)(2,1)S(1)}, u32[]{:S(2)}, u32[]{:S(2)}) %collective-permute-start.3) | collective-permute-done | bytes 131104 | tf_op jit(solution)/shard_map/ppermute | solution.py:10
  29.6 0.2 convolution_convert_fusion.1
  29.9 1.6 %collective-permute-start.4 = (bf16[64,1024]{1,0:T(8,128)(2,1)S(1)}, bf16[64,1024]{1,0:T(8,128)(2,1)S(1)}, u32[]{:S(2)}, u32[]{:S(2)}) collective-permute-start(bf16[64,1024]{1,0:T(8,128)(2,1)S(1)} %convolution_convert_fusion.1), channel_id=1, source_target_pairs={{0,16},{8,24},{16,0},{24,8},{1,17},{9,25},{17,1},{25,9},{2,18},{10... | collective-permute-start | bytes 393224 | tf_op jit(solution)/shard_map/ppermute | solution.py:10
  31.5 3.4 %collective-permute-done.4 = bf16[64,1024]{1,0:T(8,128)(2,1)S(1)} collective-permute-done((bf16[64,1024]{1,0:T(8,128)(2,1)S(1)}, bf16[64,1024]{1,0:T(8,128)(2,1)S(1)}, u32[]{:S(2)}, u32[]{:S(2)}) %collective-permute-start.4) | collective-permute-done | bytes 131104 | tf_op jit(solution)/shard_map/ppermute | solution.py:10
  34.9 0.2 multiply_reduce_fusion.1
  35.1 11.3 %add_reduce_fusion = f32[5120]{0:T(1024)S(1)} fusion(f32[384]{0:T(512)S(1)} %multiply_reduce_fusion.1, f32[5120]{0:T(1024)S(1)} %multiply_reduce_fusion, bf16[384,1024]{1,0:T(8,128)(2,1)S(1)} %constant_dynamic-update-slice_fusion, bf16[5120,1024]{1,0:T(8,128)(2,1)} %param.3), kind=kOutput, calls=%fused_computation.1 | convolution fusion | flops 4034391040 | bytes 11314688 | tf_op jit(solution)/shard_map/dot_general | solution.py:16
  46.5 1.2 %fusion.48 = (f32[]{:T(128)}, f32[5120]{0:T(1024)}) fusion(f32[5120]{0:T(1024)S(1)} %add_reduce_fusion), kind=kLoop, calls=%fused_computation.80 | loop fusion | flops 10239 | bytes 40964 | tf_op jit(solution)/shard_map/reduce_max | solution.py:74
  47.7 0.6 broadcast_in_dim.2
  48.4 0.1 collective-permute-start.5
  48.4 1.2 %collective-permute-done.5 = f32[8,128]{1,0:T(8,128)S(1)} collective-permute-done((f32[8,128]{1,0:T(8,128)S(1)}, f32[8,128]{1,0:T(8,128)S(1)}, u32[]{:S(2)}, u32[]{:S(2)}) %collective-permute-start.5) | collective-permute-done | bytes 4128 | tf_op jit(solution)/shard_map/ppermute | solution.py:79
  49.6 0.6 %broadcast_maximum_fusion = f32[8,128]{1,0:T(8,128)S(1)} fusion(f32[8,128]{1,0:T(8,128)S(1)} %collective-permute-done.5, f32[]{:T(128)} %get-tuple-element.3), kind=kLoop, calls=%fused_computation.64 | loop fusion | flops 1024 | bytes 8196 | tf_op jit(solution)/shard_map/max | solution.py:79
  50.2 1.4 %collective-permute-start.6 = (f32[8,128]{1,0:T(8,128)S(1)}, f32[8,128]{1,0:T(8,128)S(1)}, u32[]{:S(2)}, u32[]{:S(2)}) collective-permute-start(f32[8,128]{1,0:T(8,128)S(1)} %broadcast_maximum_fusion), channel_id=1, source_target_pairs={{0,3},{1,2},{2,1},{3,0},{4,7},{5,6},{6,5},{7,4},{8,11},{9,10},{10,... | collective-permute-start | bytes 12296 | tf_op jit(solution)/shard_map/ppermute | solution.py:79
  51.7 1.7 %collective-permute-done.6 = f32[8,128]{1,0:T(8,128)S(1)} collective-permute-done((f32[8,128]{1,0:T(8,128)S(1)}, f32[8,128]{1,0:T(8,128)S(1)}, u32[]{:S(2)}, u32[]{:S(2)}) %collective-permute-start.6) | collective-permute-done | bytes 4128 | tf_op jit(solution)/shard_map/ppermute | solution.py:79
  53.3 0.6 %fusion.52 = f32[8,128]{1,0:T(8,128)S(1)} fusion(f32[8,128]{1,0:T(8,128)S(1)} %collective-permute-done.6, f32[8,128]{1,0:T(8,128)S(1)} %collective-permute-done.5, f32[]{:T(128)} %get-tuple-element.3), kind=kLoop, calls=%fused_computation.81 | loop fusion | flops 2048 | bytes 12292 | tf_op jit(solution)/shard_map/max | solution.py:79
  54.0 2.1 %collective-permute-start.7 = (f32[8,128]{1,0:T(8,128)S(1)}, f32[8,128]{1,0:T(8,128)S(1)}, u32[]{:S(2)}, u32[]{:S(2)}) collective-permute-start(f32[8,128]{1,0:T(8,128)S(1)} %fusion.52), channel_id=1, source_target_pairs={{0,5},{1,4},{2,7},{3,6},{4,1},{5,0},{6,3},{7,2},{8,13},{9,12},{10,... | collective-permute-start | bytes 12296 | tf_op jit(solution)/shard_map/ppermute | solution.py:79
  56.1 1.9 %collective-permute-done.7 = f32[8,128]{1,0:T(8,128)S(1)} collective-permute-done((f32[8,128]{1,0:T(8,128)S(1)}, f32[8,128]{1,0:T(8,128)S(1)}, u32[]{:S(2)}, u32[]{:S(2)}) %collective-permute-start.7) | collective-permute-done | bytes 4128 | tf_op jit(solution)/shard_map/ppermute | solution.py:79
  58.0 1.3 %collective-permute-start.8 = (f32[8,128]{1,0:T(8,128)S(1)}, f32[8,128]{1,0:T(8,128)S(1)}, u32[]{:S(2)}, u32[]{:S(2)}) collective-permute-start(f32[8,128]{1,0:T(8,128)S(1)} %max.17), channel_id=1, source_target_pairs={{0,9},{1,8},{2,11},{3,10},{4,13},{5,12},{6,15},{7,14},{8,1},{9,0},... | collective-permute-start | bytes 12296 | tf_op jit(solution)/shard_map/ppermute | solution.py:79
  59.3 1.8 %collective-permute-done.8 = f32[8,128]{1,0:T(8,128)S(1)} collective-permute-done((f32[8,128]{1,0:T(8,128)S(1)}, f32[8,128]{1,0:T(8,128)S(1)}, u32[]{:S(2)}, u32[]{:S(2)}) %collective-permute-start.8) | collective-permute-done | bytes 4128 | tf_op jit(solution)/shard_map/ppermute | solution.py:79
  61.0 1.3 %collective-permute-start.9 = (f32[8,128]{1,0:T(8,128)S(1)}, f32[8,128]{1,0:T(8,128)S(1)}, u32[]{:S(2)}, u32[]{:S(2)}) collective-permute-start(f32[8,128]{1,0:T(8,128)S(1)} %max.18), channel_id=1, source_target_pairs={{0,17},{1,16},{2,19},{3,18},{4,21},{5,20},{6,23},{7,22},{8,25},{9,... | collective-permute-start | bytes 12296 | tf_op jit(solution)/shard_map/ppermute | solution.py:79
  62.3 0.9 %convolution_convert_fusion = bf16[64,1024]{1,0:T(8,128)(2,1)} fusion(bf16[64,1024]{1,0:T(8,128)(2,1)S(1)} %collective-permute-done.4, bf16[64,1024]{1,0:T(8,128)(2,1)S(1)} %convolution_convert_fusion.1, pred[]{:T(512)S(6)} %eq.78, s32[64]{0:T(128)S(1)} %get-tuple-element.5), kind=kOutput, calls=%fused_computation.5 | convolution fusion | flops 18030592 | bytes 393473 | tf_op jit(solution)/shard_map/dot_general | solution.py:25
  63.2 0.9 %collective-permute-done.9 = f32[8,128]{1,0:T(8,128)S(1)} collective-permute-done((f32[8,128]{1,0:T(8,128)S(1)}, f32[8,128]{1,0:T(8,128)S(1)}, u32[]{:S(2)}, u32[]{:S(2)}) %collective-permute-start.9) | collective-permute-done | bytes 4128 | tf_op jit(solution)/shard_map/ppermute | solution.py:79
  64.1 0.5 slice.3
  (8 shorter events, 0.1 us)
Async XLA Ops:
  6.6 1.5 %collective-permute-start = (bf16[64,1024]{1,0:T(8,128)(2,1)S(1)}, bf16[64,1024]{1,0:T(8,128)(2,1)S(1)}, u32[]{:S(2)}, u32[]{:S(2)}) collective-permute-start(bf16[64,1024]{1,0:T(8,128)(2,1)S(1)} %get-tuple-element.11), channel_id=1, source_target_pairs={{0,1},{1,0},{2,3},{3,2},{4,5},{5,4},{6,7},{7,6},{8,9},{9,8},{10,11... | collective-permute-start | bytes 393224 | tf_op jit(solution)/shard_map/ppermute | solution.py:10
  8.4 6.8 %collective-permute-start.1 = (bf16[64,1024]{1,0:T(8,128)(2,1)S(1)}, bf16[64,1024]{1,0:T(8,128)(2,1)S(1)}, u32[]{:S(2)}, u32[]{:S(2)}) collective-permute-start(bf16[64,1024]{1,0:T(8,128)(2,1)S(1)} %convolution_convert_fusion.4), channel_id=1, source_target_pairs={{0,2},{1,3},{2,0},{3,1},{4,6},{5,7},{6,4},{7,5},{8,10},{9,11},{10,... | collective-permute-start | bytes 393224 | tf_op jit(solution)/shard_map/ppermute | solution.py:10
  15.4 8.9 %collective-permute-start.2 = (bf16[64,1024]{1,0:T(8,128)(2,1)S(1)}, bf16[64,1024]{1,0:T(8,128)(2,1)S(1)}, u32[]{:S(2)}, u32[]{:S(2)}) collective-permute-start(bf16[64,1024]{1,0:T(8,128)(2,1)S(1)} %convolution_convert_fusion.3), channel_id=1, source_target_pairs={{0,4},{1,5},{2,6},{3,7},{4,0},{5,1},{6,2},{7,3},{8,12},{9,13},{10,... | collective-permute-start | bytes 393224 | tf_op jit(solution)/shard_map/ppermute | solution.py:10
  24.6 5.0 %collective-permute-start.3 = (bf16[64,1024]{1,0:T(8,128)(2,1)S(1)}, bf16[64,1024]{1,0:T(8,128)(2,1)S(1)}, u32[]{:S(2)}, u32[]{:S(2)}) collective-permute-start(bf16[64,1024]{1,0:T(8,128)(2,1)S(1)} %convolution_convert_fusion.2), channel_id=1, source_target_pairs={{0,8},{8,0},{16,24},{24,16},{1,9},{9,1},{17,25},{25,17},{2,10},{10... | collective-permute-start | bytes 393224 | tf_op jit(solution)/shard_map/ppermute | solution.py:10
  29.9 5.0 %collective-permute-start.4 = (bf16[64,1024]{1,0:T(8,128)(2,1)S(1)}, bf16[64,1024]{1,0:T(8,128)(2,1)S(1)}, u32[]{:S(2)}, u32[]{:S(2)}) collective-permute-start(bf16[64,1024]{1,0:T(8,128)(2,1)S(1)} %convolution_convert_fusion.1), channel_id=1, source_target_pairs={{0,16},{8,24},{16,0},{24,8},{1,17},{9,25},{17,1},{25,9},{2,18},{10... | collective-permute-start | bytes 393224 | tf_op jit(solution)/shard_map/ppermute | solution.py:10
  48.4 1.2 %collective-permute-start.5 = (f32[8,128]{1,0:T(8,128)S(1)}, f32[8,128]{1,0:T(8,128)S(1)}, u32[]{:S(2)}, u32[]{:S(2)}) collective-permute-start(f32[8,128]{1,0:T(8,128)S(1)} %broadcast_in_dim.2), channel_id=1, source_target_pairs={{0,1},{1,0},{2,3},{3,2},{4,5},{5,4},{6,7},{7,6},{8,9},{9,8},{10,11... | collective-permute-start | bytes 12296 | tf_op jit(solution)/shard_map/ppermute | solution.py:79
  50.2 3.1 %collective-permute-start.6 = (f32[8,128]{1,0:T(8,128)S(1)}, f32[8,128]{1,0:T(8,128)S(1)}, u32[]{:S(2)}, u32[]{:S(2)}) collective-permute-start(f32[8,128]{1,0:T(8,128)S(1)} %broadcast_maximum_fusion), channel_id=1, source_target_pairs={{0,3},{1,2},{2,1},{3,0},{4,7},{5,6},{6,5},{7,4},{8,11},{9,10},{10,... | collective-permute-start | bytes 12296 | tf_op jit(solution)/shard_map/ppermute | solution.py:79
  54.0 4.0 %collective-permute-start.7 = (f32[8,128]{1,0:T(8,128)S(1)}, f32[8,128]{1,0:T(8,128)S(1)}, u32[]{:S(2)}, u32[]{:S(2)}) collective-permute-start(f32[8,128]{1,0:T(8,128)S(1)} %fusion.52), channel_id=1, source_target_pairs={{0,5},{1,4},{2,7},{3,6},{4,1},{5,0},{6,3},{7,2},{8,13},{9,12},{10,... | collective-permute-start | bytes 12296 | tf_op jit(solution)/shard_map/ppermute | solution.py:79
  58.0 3.0 %collective-permute-start.8 = (f32[8,128]{1,0:T(8,128)S(1)}, f32[8,128]{1,0:T(8,128)S(1)}, u32[]{:S(2)}, u32[]{:S(2)}) collective-permute-start(f32[8,128]{1,0:T(8,128)S(1)} %max.17), channel_id=1, source_target_pairs={{0,9},{1,8},{2,11},{3,10},{4,13},{5,12},{6,15},{7,14},{8,1},{9,0},... | collective-permute-start | bytes 12296 | tf_op jit(solution)/shard_map/ppermute | solution.py:79
  61.0 3.0 %collective-permute-start.9 = (f32[8,128]{1,0:T(8,128)S(1)}, f32[8,128]{1,0:T(8,128)S(1)}, u32[]{:S(2)}, u32[]{:S(2)}) collective-permute-start(f32[8,128]{1,0:T(8,128)S(1)} %max.18), channel_id=1, source_target_pairs={{0,17},{1,16},{2,19},{3,18},{4,21},{5,20},{6,23},{7,22},{8,25},{9,... | collective-permute-start | bytes 12296 | tf_op jit(solution)/shard_map/ppermute | solution.py:79

commit v2 on v1

v2 whole, which is shorter than its diff:
```python
import functools

import jax
import jax.numpy as jnp
from jax import lax
from jax.experimental import pallas as pl
from jax.experimental.pallas import tpu as pltpu
from jax.sharding import PartitionSpec as P


GROUP = 8
CHUNK = 256
FAR = 3.0e38
NT = (((1,), (1,)), ((), ()))
VMEM = pl.BlockSpec(memory_space=pltpu.VMEM)


def cost(flops):
    return pl.CostEstimate(flops=flops, bytes_accessed=2**20, transcendentals=0)


def gather_kernel(picks_ref, points_ref, out_ref, held, sem):
    count = out_ref.shape[0]
    copies = []
    for i in range(count):
        start = pl.multiple_of(picks_ref[0, i] // GROUP * GROUP, GROUP)
        copies.append(
            pltpu.make_async_copy(
                points_ref.at[pl.ds(start, GROUP), :],
                held.at[pl.ds(i * GROUP, GROUP), :],
                sem.at[i],
            )
        )
        copies[-1].start()
    down = lax.broadcasted_iota(jnp.int32, (count, 128), 0)
    wanted = down * GROUP
    for i in range(count):
        wanted = jnp.where(down == i, wanted + lax.rem(picks_ref[0, i], GROUP), wanted)
    lanes = lax.broadcasted_iota(jnp.int32, (count, 128), 1)
    onehot = jnp.concatenate(
        [(lanes + base == wanted).astype(jnp.bfloat16) for base in range(0, count * GROUP, 128)],
        axis=1,
    )
    for copy in copies:
        copy.wait()
    out_ref[...] = jnp.dot(
        onehot, held[...], preferred_element_type=jnp.float32
    ).astype(jnp.bfloat16)


def gather_rows(points, picks):
    count = picks.shape[1]
    width = points.shape[1]
    return pl.pallas_call(
        gather_kernel,
        out_shape=pltpu.VMEM((count, width), points.dtype),
        in_specs=[
            pl.BlockSpec(memory_space=pltpu.SMEM),
            pl.BlockSpec(memory_space=pltpu.HBM),
        ],
        out_specs=VMEM,
        scratch_shapes=[
            pltpu.VMEM((count * GROUP, width), points.dtype),
            pltpu.SemaphoreType.DMA((count,)),
        ],
        compiler_params=pltpu.CompilerParams(vmem_limit_bytes=56 * 2**20),
        cost_estimate=cost(10**9),
        name="gather_rows",
    )(picks, points)


def swap_halves(index, count, lower):
    swapped_index = jnp.where(index < count, index + count, index - count)
    return jnp.where(lower, index, swapped_index)


def upright(row):
    size = row.shape[1]
    across = lax.broadcasted_iota(jnp.int32, (size, size), 1)
    down = lax.broadcasted_iota(jnp.int32, (size, size), 0)
    spread = jnp.where(across == down, jnp.broadcast_to(row, (size, size)), 0)
    return jnp.sum(spread.astype(jnp.float32), axis=1, keepdims=True).astype(jnp.int32)


def plan_kernel(phases, count, devices, picks_ref, *out_refs):
    number = lax.axis_index("gx") * lax.axis_size("gy") + lax.axis_index("gy")
    outs = list(out_refs)
    north = (number & 1) == 1

    def row_of(step, place):
        return picks_ref[pl.ds(devices - (devices >> step) + (place >> step + 1), 1), :]

    def onehot(column, total):
        lanes = lax.broadcasted_iota(jnp.int32, (count, total), 1)
        return (lanes == column).astype(jnp.bfloat16)

    for step, kind in phases:
        lower = (number >> step & 1) == 0
        own = swap_halves(row_of(step, number), count, lower)
        if kind == "single":
            outs.pop(0)[...] = onehot(upright(own), 2 * count)
            continue
        beside = swap_halves(row_of(step, number ^ 2 << step), count, lower)
        lower_next = (number >> step + 1 & 1) == 0
        top = upright(swap_halves(row_of(step + 1, number), count, lower_next))
        lanes = lax.broadcasted_iota(jnp.int32, (count, count), 1)
        relative = jnp.where(lanes == top, own, 0) + jnp.where(
            lanes + count == top, beside + 2 * count, 0
        )
        relative = jnp.sum(relative.astype(jnp.float32), axis=1, keepdims=True)
        relative = relative.astype(jnp.int32)
        spot = lax.broadcasted_iota(jnp.int32, (3 * count, 1), 0) + count
        if kind == "mixed":
            half = count // 2
            near = jnp.where(north, 3 * half, 0)
            far = jnp.where(north, 0, 3 * half)
            back = relative - 2 * count
            first = jnp.where(north, 0, 3 * half)
            last = jnp.where(north, 3 * half, 0) - half
            place = jnp.where(
                relative < count,
                relative,
                jnp.where(
                    relative < 2 * count,
                    relative + near,
                    jnp.where(
                        relative < 3 * count,
                        back + 2 * count + jnp.where(back < half, first, last),
                        relative - 2 * count + far,
                    ),
                ),
            )
            inside = spot - count
            second = inside >= 3 * half
            inside = jnp.where(second, inside - 3 * half, inside)
            mine = second ^ north
            spot = jnp.where(
                inside < count,
                jnp.where(mine, inside + 3 * count, inside + count),
                jnp.where(mine, inside + count, inside + count + half),
            )
        else:
            place = relative
        outs.pop(0)[...] = onehot(place, 4 * count)
        kept = jnp.where(spot - 2 * count == beside, 1.0, 0.0)
        kept = jnp.max(kept, axis=1, keepdims=True)
        kept = jnp.where(spot < 2 * count, 1.0, kept)
        outs.pop(0)[...] = jnp.where(kept > 0.5, 0.0, FAR)


def make_plan(picks, phases, devices):
    count = picks.shape[1]
    shapes = []
    for _, kind in phases:
        if kind == "single":
            shapes.append(pltpu.VMEM((count, 2 * count), jnp.bfloat16))
        else:
            shapes.append(pltpu.VMEM((count, 4 * count), jnp.bfloat16))
            shapes.append(pltpu.VMEM((3 * count, 1), jnp.float32))
    return pl.pallas_call(
        functools.partial(plan_kernel, phases, count, devices),
        out_shape=tuple(shapes),
        in_specs=[VMEM],
        out_specs=(VMEM,) * len(shapes),
        compiler_params=pltpu.CompilerParams(vmem_limit_bytes=4 * 2**20),
        cost_estimate=pl.CostEstimate(flops=10**10, bytes_accessed=2**27, transcendentals=0),
        name="plan",
    )(picks)


def weights_of(refs, penalty_ref=None):
    value = refs[0][...] if len(refs) == 1 else jnp.concatenate([r[...] for r in refs], 0)
    wide = value.astype(jnp.float32)
    top = jnp.sum(wide * wide, axis=1, keepdims=True)
    if penalty_ref is not None:
        top = top + penalty_ref[...]
    return value * jnp.bfloat16(-2.0), top


def score_kernel(number, masked, first, last, held_ref, *refs):
    rows, width = held_ref.shape
    sets = refs[:number]
    rest = list(refs[number:])
    penalty_ref = rest.pop(0) if masked else None
    if not first:
        before_ref, squares_ref = rest.pop(0), rest.pop(0)
    out_ref = rest.pop(0)
    weight, top = weights_of(sets, penalty_ref)
    ones = jnp.ones((8, 128), jnp.bfloat16)
    peak = None
    for piece in range(rows // CHUNK):
        window = pl.ds(piece * CHUNK, CHUNK)
        value = held_ref[window, :]
        part = lax.dot_general(weight, value, NT, preferred_element_type=jnp.float32)
        least = jnp.min(part + top, axis=0, keepdims=True)
        if first:
            block = value.astype(jnp.float32)
            block = block * block
            partial = block[:, :128]
            for lane in range(128, width, 128):
                partial = partial + block[:, lane : lane + 128]
            high = partial.astype(jnp.bfloat16)
            low = (partial - high.astype(jnp.float32)).astype(jnp.bfloat16)
            total = lax.dot_general(
                ones, high, NT, preferred_element_type=jnp.float32
            ) + lax.dot_general(ones, low, NT, preferred_element_type=jnp.float32)
            rest[0][:, window] = total[:1, :]
        else:
            least = jnp.minimum(least, before_ref[:, window])
        if last:
            least = (least + squares_ref[:, window]) / width
            peak = least if peak is None else jnp.maximum(peak, least)
        out_ref[:, window] = least
    if last:
        rest[0][...] = jnp.broadcast_to(jnp.max(peak, axis=1, keepdims=True), rest[0].shape)


def score(held, sets, penalty, before=None, squares=None, last=False):
    rows = held.shape[0]
    masked = penalty is not None
    first = before is None
    operands = [held, *sets] + ([penalty] if masked else [])
    out_shape = [pltpu.VMEM((1, rows), jnp.float32)]
    if first:
        out_shape.append(pltpu.VMEM((1, rows), jnp.float32))
    else:
        operands += [before, squares]
    if last:
        out_shape.append(pltpu.VMEM((8, 128), jnp.float32))
    return pl.pallas_call(
        functools.partial(score_kernel, len(sets), masked, first, last),
        out_shape=tuple(out_shape),
        in_specs=[VMEM] * len(operands),
        out_specs=(VMEM,) * len(out_shape),
        compiler_params=pltpu.CompilerParams(vmem_limit_bytes=16 * 2**20),
        cost_estimate=cost(3 * 10**9),
        name="score_first" if first else "score_last" if last else "score",
    )(*operands)


def choose(onehot, held):
    rows = held[0] if len(held) == 1 else jnp.concatenate(held, 0)
    return jnp.dot(onehot, rows, preferred_element_type=jnp.float32).astype(rows.dtype)


def phase_spans(size_gx, size_gy):
    bits_gy = size_gy.bit_length() - 1
    rounds = bits_gy + size_gx.bit_length() - 1
    spans = [(0, 1)]
    for begin, end in ((1, bits_gy), (bits_gy, rounds)):
        for step in range(begin, end, 2):
            spans.append((step, min(step + 2, end)))
    return spans


def per_device(embeddings, device_local_selections, merge_picks):
    count = device_local_selections.shape[1]
    size_gx = lax.axis_size("gx")
    size_gy = lax.axis_size("gy")
    devices = size_gx * size_gy
    number = lax.axis_index("gx") * size_gy + lax.axis_index("gy")
    north = (number & 1) == 1

    def swap(value, mask, other=None):
        other = mask if other is None else other
        pairs = [(source, source ^ (mask if source & 1 else other)) for source in range(devices)]
        return lax.ppermute(value, ("gx", "gy"), pairs)

    phases = []
    for begin, end in phase_spans(size_gx, size_gy):
        kind = "mixed" if end <= size_gy.bit_length() - 1 else "plain"
        phases.append((begin, kind if end - begin > 1 else "single"))

    sets = gather_rows(embeddings, device_local_selections)
    plan = list(make_plan(merge_picks, phases, devices))
    cover = None
    pending = None
    for step, kind in phases:
        near, high = 1 << step, 2 << step
        onehot = plan.pop(0)
        if kind == "single":
            penalty = None
            others = [swap(sets, near)]
        else:
            penalty = plan.pop(0)
            if kind == "mixed":
                half = count // 2
                part = jnp.where(north, sets[:half], sets[half:])
                first = swap(sets, near | high, near)
                second = swap(part, high)
                here = jnp.concatenate([first, second], 0)
                others = [here, swap(here, 1)]
            else:
                others = [swap(sets, near)]
                others.append(swap(sets, high))
                others.append(swap(sets, near | high))
        if pending is not None:
            if cover is None:
                cover, squares = score(embeddings, *pending)
            else:
                cover, = score(embeddings, *pending, cover, squares)
        pending = ([sets] if step == 0 else []) + others, penalty
        sets = choose(onehot, [sets] + others)
    cover, peak = score(embeddings, *pending, cover, squares, last=True)
    bit = 1
    while bit < devices:
        peak = jnp.maximum(peak, swap(peak, bit | 1))
        bit *= 2
    return (sets, cover[0], peak[0, 0])


def solution(mesh):
    return jax.shard_map(
        per_device,
        mesh=mesh,
        in_specs=(P(("gx", "gy"), None), P(("gx", "gy"), None), P()),
        out_specs=(P(), P(("gx", "gy")), P()),
        check_vma=False,
    )
```

time: 64.9 us -> 53.9 us (0.83)
  matrix products: 19.1 us -> 1.25 us
  Pallas kernels: 0 us -> 14.2 us
  other arithmetic: 8.84 us -> 0.03 us
  local copies, waits for them, and re-layouts: 2.02 us -> 9.1 us
  waiting for transfers between devices: 18.2 us -> 14.5 us
  starting transfers between devices: 15.6 us -> 13.7 us
    dot_general x7 -> x3, matrix products: 19.1 us -> 1.25 us  [choose(): jnp.dot(onehot, rows, preferred_element_type=jnp.float32).astype(rows.dtype)]
    pallas_call x0 -> x5, Pallas kernels: none -> 14.2 us  [the longest x3 11.1 us: score(): pl.pallas_call(functools.partial(score_kernel, len(sets), masked, first,...]
    unnamed x4 -> x8, local copies, waits for them, and re-layouts: 0.04 us -> 8.58 us
    reduce_sum x2 -> x0, other arithmetic: 6.33 us -> none  [the longest x1 6.09 us: per_device(): squares = jnp.sum(wide * wide, axis=1)]
    ppermute x10 -> x12, waiting for transfers between devices: 18.2 us -> 14.5 us  [swap(): return lax.ppermute(value, ('gx', 'gy'), pairs)]
    ppermute x10 -> x12, starting transfers between devices: 15.6 us -> 13.7 us  [swap(): return lax.ppermute(value, ('gx', 'gy'), pairs)]
    max x5, other arithmetic: 1.31 us -> 0.02 us  [per_device(): peak = jnp.maximum(peak, swap(peak, bit | 1))]
    reduce_max x1 -> x0, other arithmetic: 1.21 us -> none  [per_device(): peak = jnp.broadcast_to(jnp.max(cover), (8, 128))]
  transfers between devices with their start and end apart: 10 -> 12, of which waited for: 9 -> 8; matrix products, arithmetic and copies ran while one was open for 12% -> 3% of each run, Pallas kernels for 0% -> 14%
where the time goes in v2:
time: 53.9 us; the launch traced here: 53.6 us
  waiting for transfers between devices  14.5 us (27%)
  Pallas kernels  14.2 us (26%)
  starting transfers between devices  13.7 us (25%)
  local copies, waits for them, and re-layouts  9.1 us (17%)
  matrix products  1.25 us (2%)
  between operations  0.75 us (1%)
    ppermute x12, waiting for transfers between devices, swap(): return lax.ppermute(value, ('gx', 'gy'), pairs)  14.5 us
    ppermute x12, starting transfers between devices, swap(): return lax.ppermute(value, ('gx', 'gy'), pairs)  13.7 us
    pallas_call x3, Pallas kernels, score(): pl.pallas_call(functools.partial(score_kernel, len(sets), masked, first,...  11.1 us
    unnamed x8, local copies, waits for them, and re-layouts  8.58 us
    pallas_call x1, Pallas kernels, gather_rows(): pl.pallas_call(gather_kernel, out_shape=pltpu.VMEM((count, width), points...  2.97 us
    dot_general x3, matrix products, choose(): jnp.dot(onehot, rows, preferred_element_type=jnp.float32).astype(rows.dtype)  1.25 us
  transfers between devices with their start and end apart: 12, of which 8 were waited for; matrix products, arithmetic and copies ran while one was open for 3% of the time, Pallas kernels for 14%

profile of v2, /device:TPU:0, one launch (start us, length us, event | category | flops | bytes accessed | tf_op | source)
XLA Modules:
  0.0 53.6 jit_solution(4427452757941384432)
XLA Ops:
  0.6 0.0 copy-start.2
  0.6 3.0 %gather_rows.1.refs_0_ = bf16[64,1024]{1,0:T(8,128)(2,1)S(1)} custom-call(s32[1,64]{1,0:T(1,128)} %picks_ref.2, bf16[5120,1024]{1,0:T(8,128)(2,1)} %held_ref.5), custom_call_target="tpu_custom_call" | custom-call | flops 1000000000 | bytes 1048576 | tf_op jit(solution)/shard_map/gather_rows/pallas_call | solution.py:54
  3.6 0.6 %collective-permute-start = (bf16[64,1024]{1,0:T(8,128)(2,1)S(1)}, bf16[64,1024]{1,0:T(8,128)(2,1)S(1)}, u32[]{:S(2)}, u32[]{:S(2)}) collective-permute-start(bf16[64,1024]{1,0:T(8,128)(2,1)S(1)} %gather_rows.1.refs_0_), channel_id=1, source_target_pairs={{0,1},{1,0},{2,3},{3,2},{4,5},{5,4},{6,7},{7,6},{8,9},{9,8},{10,11... | collective-permute-start | bytes 393224 | tf_op jit(solution)/shard_map/ppermute | solution.py:267
  4.2 0.0 copy-done.2
  4.2 0.2 plan.1
  4.4 0.8 %collective-permute-done.refs_1_ = bf16[64,1024]{1,0:T(8,128)(2,1)S(1)} collective-permute-done((bf16[64,1024]{1,0:T(8,128)(2,1)S(1)}, bf16[64,1024]{1,0:T(8,128)(2,1)S(1)}, u32[]{:S(2)}, u32[]{:S(2)}) %collective-permute-start) | collective-permute-done | bytes 131104 | tf_op jit(solution)/shard_map/ppermute | solution.py:267
  5.2 0.2 fusion.2
  5.3 3.0 %collective-permute-start.1 = (bf16[64,1024]{1,0:T(8,128)(2,1)S(1)}, bf16[64,1024]{1,0:T(8,128)(2,1)S(1)}, u32[]{:S(2)}, u32[]{:S(2)}) collective-permute-start(bf16[64,1024]{1,0:T(8,128)(2,1)S(1)} %fusion.2), channel_id=1, source_target_pairs={{0,2},{1,7},{2,0},{3,5},{4,6},{5,3},{6,4},{7,1},{8,10},{9,15},{10,... | collective-permute-start | bytes 393224 | tf_op jit(solution)/shard_map/ppermute | solution.py:267
  8.3 2.7 %collective-permute-start.2 = (bf16[32,1024]{1,0:T(8,128)(2,1)S(1)}, bf16[32,1024]{1,0:T(8,128)(2,1)S(1)}, u32[]{:S(2)}, u32[]{:S(2)}) collective-permute-start(bf16[32,1024]{1,0:T(8,128)(2,1)S(1)} %slice_select_fusion), channel_id=1, source_target_pairs={{0,4},{1,5},{2,6},{3,7},{4,0},{5,1},{6,2},{7,3},{8,12},{9,13},{10,... | collective-permute-start | bytes 196616 | tf_op jit(solution)/shard_map/ppermute | solution.py:267
  11.0 0.3 collective-permute-done.1
  11.3 4.6 %collective-permute-done.2 = bf16[32,1024]{1,0:T(8,128)(2,1)S(1)} collective-permute-done((bf16[32,1024]{1,0:T(8,128)(2,1)S(1)}, bf16[32,1024]{1,0:T(8,128)(2,1)S(1)}, u32[]{:S(2)}, u32[]{:S(2)}) %collective-permute-start.2) | collective-permute-done | bytes 65568 | tf_op jit(solution)/shard_map/ppermute | solution.py:267
  15.9 0.1 collective-permute-start.3
  16.0 0.0 copy-start
  16.0 4.0 %copy-done = bf16[5120,1024]{1,0:T(8,128)(2,1)S(1)} copy-done((bf16[5120,1024]{1,0:T(8,128)(2,1)S(1)}, bf16[5120,1024]{1,0:T(8,128)(2,1)}, u32[]{:S(2)}) %copy-start) | copy-done | bytes 10485784
  20.0 3.9 %score_first.1 = (f32[1,5120]{1,0:T(1,128)S(1)}, f32[1,5120]{1,0:T(1,128)S(1)}) custom-call(bf16[5120,1024]{1,0:T(8,128)(2,1)S(1)} %copy-done, bf16[64,1024]{1,0:T(8,128)(2,1)S(1)} %gather_rows.1.refs_0_, bf16[64,1024]{1,0:T(8,128)(2,1)S(1)} %collective-permute-done.refs_1_), custom_call_target="tpu_custom_call" | custom-call | flops 3000000000 | bytes 1048576 | tf_op jit(solution)/shard_map/score_first/pallas_call | solution.py:230
  23.8 0.0 collective-permute-done.3.refs_1_
  23.9 0.2 fusion
  24.1 2.5 %collective-permute-start.6 = (bf16[64,1024]{1,0:T(8,128)(2,1)S(1)}, bf16[64,1024]{1,0:T(8,128)(2,1)S(1)}, u32[]{:S(2)}, u32[]{:S(2)}) collective-permute-start(bf16[64,1024]{1,0:T(8,128)(2,1)S(1)} %fusion), channel_id=1, source_target_pairs={{0,24},{1,25},{2,26},{3,27},{4,28},{5,29},{6,30},{7,31},{8,16},{9,... | collective-permute-start | bytes 393224 | tf_op jit(solution)/shard_map/ppermute | solution.py:267
  26.6 0.5 collective-permute-start.5
  27.1 0.5 %collective-permute-start.4 = (bf16[64,1024]{1,0:T(8,128)(2,1)S(1)}, bf16[64,1024]{1,0:T(8,128)(2,1)S(1)}, u32[]{:S(2)}, u32[]{:S(2)}) collective-permute-start(bf16[64,1024]{1,0:T(8,128)(2,1)S(1)} %fusion), channel_id=1, source_target_pairs={{0,8},{1,9},{2,10},{3,11},{4,12},{5,13},{6,14},{7,15},{8,0},{9,1},... | collective-permute-start | bytes 393224 | tf_op jit(solution)/shard_map/ppermute | solution.py:267
  27.6 0.0 copy-start.1
  27.6 4.0 %copy-done.1 = bf16[5120,1024]{1,0:T(8,128)(2,1)S(1)} copy-done((bf16[5120,1024]{1,0:T(8,128)(2,1)S(1)}, bf16[5120,1024]{1,0:T(8,128)(2,1)}, u32[]{:S(2)}) %copy-start.1) | copy-done | bytes 10485784
  31.6 3.6 %score.1.refs_4_ = f32[1,5120]{1,0:T(1,128)S(1)} custom-call(bf16[5120,1024]{1,0:T(8,128)(2,1)S(1)} %copy-done.1, bf16[96,1024]{1,0:T(8,128)(2,1)S(1)} %constant_dynamic-update-slice_fusion.refs_0_, bf16[96,1024]{1,0:T(8,128)(2,1)S(1)} %collective-permute-done.3.refs_1_, f32[192,1]{1,0:T(8,128)S(1)} %get-tuple-element.16.refs_2_, ...), custom_call_target="tpu_custom_call" | custom-call | flops 3000000000 | bytes 1048576 | tf_op jit(solution)/shard_map/score/pallas_call | solution.py:230
  35.2 0.0 collective-permute-done.6.refs_2_
  35.2 0.0 collective-permute-done.5.refs_1_
  35.2 0.0 collective-permute-done.4.refs_0_
  35.2 3.6 %score_last.1 = (f32[1,5120]{1,0:T(1,128)S(1)}, f32[8,128]{1,0:T(8,128)S(1)}) custom-call(bf16[5120,1024]{1,0:T(8,128)(2,1)S(1)} %copy-done.1, bf16[64,1024]{1,0:T(8,128)(2,1)S(1)} %collective-permute-done.4.refs_0_, bf16[64,1024]{1,0:T(8,128)(2,1)S(1)} %collective-permute-done.5.refs_1_, bf16[64,1024]{1,0:T(8,128)(2,1)S(1)} %collective-permute-done.6.refs_2_, ...), custom_call_target="tpu_custom_call" | custom-call | flops 3000000000 | bytes 1048576 | tf_op jit(solution)/shard_map/score_last/pallas_call | solution.py:230
  38.8 0.0 collective-permute-start.7
  38.8 1.2 %collective-permute-done.7 = f32[8,128]{1,0:T(8,128)S(1)} collective-permute-done((f32[8,128]{1,0:T(8,128)S(1)}, f32[8,128]{1,0:T(8,128)S(1)}, u32[]{:S(2)}, u32[]{:S(2)}) %collective-permute-start.7) | collective-permute-done | bytes 4128 | tf_op jit(solution)/shard_map/ppermute | solution.py:267
  40.0 0.0 collective-permute-start.8
  40.0 3.0 %collective-permute-done.8 = f32[8,128]{1,0:T(8,128)S(1)} collective-permute-done((f32[8,128]{1,0:T(8,128)S(1)}, f32[8,128]{1,0:T(8,128)S(1)}, u32[]{:S(2)}, u32[]{:S(2)}) %collective-permute-start.8) | collective-permute-done | bytes 4128 | tf_op jit(solution)/shard_map/ppermute | solution.py:267
  43.0 1.2 %collective-permute-start.9 = (f32[8,128]{1,0:T(8,128)S(1)}, f32[8,128]{1,0:T(8,128)S(1)}, u32[]{:S(2)}, u32[]{:S(2)}) collective-permute-start(f32[8,128]{1,0:T(8,128)S(1)} %max.16), channel_id=1, source_target_pairs={{0,5},{1,4},{2,7},{3,6},{4,1},{5,0},{6,3},{7,2},{8,13},{9,12},{10,... | collective-permute-start | bytes 12296 | tf_op jit(solution)/shard_map/ppermute | solution.py:267
  44.3 2.7 %collective-permute-done.9 = f32[8,128]{1,0:T(8,128)S(1)} collective-permute-done((f32[8,128]{1,0:T(8,128)S(1)}, f32[8,128]{1,0:T(8,128)S(1)}, u32[]{:S(2)}, u32[]{:S(2)}) %collective-permute-start.9) | collective-permute-done | bytes 4128 | tf_op jit(solution)/shard_map/ppermute | solution.py:267
  47.0 1.3 %collective-permute-start.10 = (f32[8,128]{1,0:T(8,128)S(1)}, f32[8,128]{1,0:T(8,128)S(1)}, u32[]{:S(2)}, u32[]{:S(2)}) collective-permute-start(f32[8,128]{1,0:T(8,128)S(1)} %max.17), channel_id=1, source_target_pairs={{0,9},{1,8},{2,11},{3,10},{4,13},{5,12},{6,15},{7,14},{8,1},{9,0},... | collective-permute-start | bytes 12296 | tf_op jit(solution)/shard_map/ppermute | solution.py:267
  48.3 1.7 %collective-permute-done.10 = f32[8,128]{1,0:T(8,128)S(1)} collective-permute-done((f32[8,128]{1,0:T(8,128)S(1)}, f32[8,128]{1,0:T(8,128)S(1)}, u32[]{:S(2)}, u32[]{:S(2)}) %collective-permute-start.10) | collective-permute-done | bytes 4128 | tf_op jit(solution)/shard_map/ppermute | solution.py:267
  50.0 1.3 %collective-permute-start.11 = (f32[8,128]{1,0:T(8,128)S(1)}, f32[8,128]{1,0:T(8,128)S(1)}, u32[]{:S(2)}, u32[]{:S(2)}) collective-permute-start(f32[8,128]{1,0:T(8,128)S(1)} %max.18), channel_id=1, source_target_pairs={{0,17},{1,16},{2,19},{3,18},{4,21},{5,20},{6,23},{7,22},{8,25},{9,... | collective-permute-start | bytes 12296 | tf_op jit(solution)/shard_map/ppermute | solution.py:267
  51.3 0.9 %fusion.1 = bf16[64,1024]{1,0:T(8,128)(2,1)} fusion(bf16[64,256]{1,0:T(8,128)(2,1)S(1)} %get-tuple-element.14, bf16[64,1024]{1,0:T(8,128)(2,1)S(1)} %collective-permute-done.6.refs_2_, bf16[64,1024]{1,0:T(8,128)(2,1)S(1)} %collective-permute-done.5.refs_1_, bf16[64,1024]{1,0:T(8,128)(2,1)S(1)} %collective-permute-done.4.refs_0_, bf16[64,1024]{1,0:T(8,128)(2,1)S(1)} %fusion), kind=kOutput, calls=%fused_computation.4 | convolution fusion | flops 35717120 | bytes 688128 | tf_op jit(solution)/shard_map/dot_general | solution.py:243
  52.2 0.6 %copy.7 = f32[5120]{0:T(1024)} copy(f32[5120]{0:T(1024)S(1)} %bitcast.11) | data formatting | bytes 40960
  52.8 0.2 collective-permute-done.11
  53.1 0.5 slice.11
  (8 shorter events, 0.0 us)
Async XLA Ops:
  0.6 3.6 %copy-start.2 = (s32[32,64]{1,0:T(8,128)S(1)}, s32[32,64]{1,0:T(8,128)}, u32[]{:S(2)}) copy-start(s32[32,64]{1,0:T(8,128)} %picks_ref.3) | copy-start | bytes 24580
  3.6 1.5 %collective-permute-start = (bf16[64,1024]{1,0:T(8,128)(2,1)S(1)}, bf16[64,1024]{1,0:T(8,128)(2,1)S(1)}, u32[]{:S(2)}, u32[]{:S(2)}) collective-permute-start(bf16[64,1024]{1,0:T(8,128)(2,1)S(1)} %gather_rows.1.refs_0_), channel_id=1, source_target_pairs={{0,1},{1,0},{2,3},{3,2},{4,5},{5,4},{6,7},{7,6},{8,9},{9,8},{10,11... | collective-permute-start | bytes 393224 | tf_op jit(solution)/shard_map/ppermute | solution.py:267
  5.3 5.9 %collective-permute-start.1 = (bf16[64,1024]{1,0:T(8,128)(2,1)S(1)}, bf16[64,1024]{1,0:T(8,128)(2,1)S(1)}, u32[]{:S(2)}, u32[]{:S(2)}) collective-permute-start(bf16[64,1024]{1,0:T(8,128)(2,1)S(1)} %fusion.2), channel_id=1, source_target_pairs={{0,2},{1,7},{2,0},{3,5},{4,6},{5,3},{6,4},{7,1},{8,10},{9,15},{10,... | collective-permute-start | bytes 393224 | tf_op jit(solution)/shard_map/ppermute | solution.py:267
  8.3 7.5 %collective-permute-start.2 = (bf16[32,1024]{1,0:T(8,128)(2,1)S(1)}, bf16[32,1024]{1,0:T(8,128)(2,1)S(1)}, u32[]{:S(2)}, u32[]{:S(2)}) collective-permute-start(bf16[32,1024]{1,0:T(8,128)(2,1)S(1)} %slice_select_fusion), channel_id=1, source_target_pairs={{0,4},{1,5},{2,6},{3,7},{4,0},{5,1},{6,2},{7,3},{8,12},{9,13},{10,... | collective-permute-start | bytes 196616 | tf_op jit(solution)/shard_map/ppermute | solution.py:267
  15.9 8.0 %collective-permute-start.3 = (bf16[96,1024]{1,0:T(8,128)(2,1)S(1)}, bf16[96,1024]{1,0:T(8,128)(2,1)S(1)}, u32[]{:S(2)}, u32[]{:S(2)}) collective-permute-start(bf16[96,1024]{1,0:T(8,128)(2,1)S(1)} %constant_dynamic-update-slice_fusion.refs_0_), channel_id=1, source_target_pairs={{0,1},{1,0},{2,3},{3,2},{4,5},{5,4},{6,7},{7,6},{8,9},{9,8},{10,11... | collective-permute-start | bytes 589832 | tf_op jit(solution)/shard_map/ppermute | solution.py:267
  16.0 4.0 %copy-start = (bf16[5120,1024]{1,0:T(8,128)(2,1)S(1)}, bf16[5120,1024]{1,0:T(8,128)(2,1)}, u32[]{:S(2)}) copy-start(bf16[5120,1024]{1,0:T(8,128)(2,1)} %held_ref.5) | copy-start | bytes 31457284
  24.1 11.1 %collective-permute-start.6 = (bf16[64,1024]{1,0:T(8,128)(2,1)S(1)}, bf16[64,1024]{1,0:T(8,128)(2,1)S(1)}, u32[]{:S(2)}, u32[]{:S(2)}) collective-permute-start(bf16[64,1024]{1,0:T(8,128)(2,1)S(1)} %fusion), channel_id=1, source_target_pairs={{0,24},{1,25},{2,26},{3,27},{4,28},{5,29},{6,30},{7,31},{8,16},{9,... | collective-permute-start | bytes 393224 | tf_op jit(solution)/shard_map/ppermute | solution.py:267
  26.6 8.6 %collective-permute-start.5 = (bf16[64,1024]{1,0:T(8,128)(2,1)S(1)}, bf16[64,1024]{1,0:T(8,128)(2,1)S(1)}, u32[]{:S(2)}, u32[]{:S(2)}) collective-permute-start(bf16[64,1024]{1,0:T(8,128)(2,1)S(1)} %fusion), channel_id=1, source_target_pairs={{0,16},{1,17},{2,18},{3,19},{4,20},{5,21},{6,22},{7,23},{8,24},{9,... | collective-permute-start | bytes 393224 | tf_op jit(solution)/shard_map/ppermute | solution.py:267
  27.1 8.1 %collective-permute-start.4 = (bf16[64,1024]{1,0:T(8,128)(2,1)S(1)}, bf16[64,1024]{1,0:T(8,128)(2,1)S(1)}, u32[]{:S(2)}, u32[]{:S(2)}) collective-permute-start(bf16[64,1024]{1,0:T(8,128)(2,1)S(1)} %fusion), channel_id=1, source_target_pairs={{0,8},{1,9},{2,10},{3,11},{4,12},{5,13},{6,14},{7,15},{8,0},{9,1},... | collective-permute-start | bytes 393224 | tf_op jit(solution)/shard_map/ppermute | solution.py:267
  27.6 4.0 %copy-start.1 = (bf16[5120,1024]{1,0:T(8,128)(2,1)S(1)}, bf16[5120,1024]{1,0:T(8,128)(2,1)}, u32[]{:S(2)}) copy-start(bf16[5120,1024]{1,0:T(8,128)(2,1)} %held_ref.5) | copy-start | bytes 31457284
  38.8 1.2 %collective-permute-start.7 = (f32[8,128]{1,0:T(8,128)S(1)}, f32[8,128]{1,0:T(8,128)S(1)}, u32[]{:S(2)}, u32[]{:S(2)}) collective-permute-start(f32[8,128]{1,0:T(8,128)S(1)} %get-tuple-element.20), channel_id=1, source_target_pairs={{0,1},{1,0},{2,3},{3,2},{4,5},{5,4},{6,7},{7,6},{8,9},{9,8},{10,11... | collective-permute-start | bytes 12296 | tf_op jit(solution)/shard_map/ppermute | solution.py:267
  40.0 3.0 %collective-permute-start.8 = (f32[8,128]{1,0:T(8,128)S(1)}, f32[8,128]{1,0:T(8,128)S(1)}, u32[]{:S(2)}, u32[]{:S(2)}) collective-permute-start(f32[8,128]{1,0:T(8,128)S(1)} %max.15), channel_id=1, source_target_pairs={{0,3},{1,2},{2,1},{3,0},{4,7},{5,6},{6,5},{7,4},{8,11},{9,10},{10,... | collective-permute-start | bytes 12296 | tf_op jit(solution)/shard_map/ppermute | solution.py:267
  43.0 3.9 %collective-permute-start.9 = (f32[8,128]{1,0:T(8,128)S(1)}, f32[8,128]{1,0:T(8,128)S(1)}, u32[]{:S(2)}, u32[]{:S(2)}) collective-permute-start(f32[8,128]{1,0:T(8,128)S(1)} %max.16), channel_id=1, source_target_pairs={{0,5},{1,4},{2,7},{3,6},{4,1},{5,0},{6,3},{7,2},{8,13},{9,12},{10,... | collective-permute-start | bytes 12296 | tf_op jit(solution)/shard_map/ppermute | solution.py:267
  47.0 3.0 %collective-permute-start.10 = (f32[8,128]{1,0:T(8,128)S(1)}, f32[8,128]{1,0:T(8,128)S(1)}, u32[]{:S(2)}, u32[]{:S(2)}) collective-permute-start(f32[8,128]{1,0:T(8,128)S(1)} %max.17), channel_id=1, source_target_pairs={{0,9},{1,8},{2,11},{3,10},{4,13},{5,12},{6,15},{7,14},{8,1},{9,0},... | collective-permute-start | bytes 12296 | tf_op jit(solution)/shard_map/ppermute | solution.py:267
  50.0 3.0 %collective-permute-start.11 = (f32[8,128]{1,0:T(8,128)S(1)}, f32[8,128]{1,0:T(8,128)S(1)}, u32[]{:S(2)}, u32[]{:S(2)}) collective-permute-start(f32[8,128]{1,0:T(8,128)S(1)} %max.18), channel_id=1, source_target_pairs={{0,17},{1,16},{2,19},{3,18},{4,21},{5,20},{6,23},{7,22},{8,25},{9,... | collective-permute-start | bytes 12296 | tf_op jit(solution)/shard_map/ppermute | solution.py:267

commit v3 on v2

--- a/solution.py
+++ b/solution.py
@@ -9,6 +9,7 @@
 
 
 GROUP = 8
+LEGS = {"gy": ("shared", "north", "south"), "gx": ("south", "shared", "north")}
 CHUNK = 256
 FAR = 3.0e38
 NT = (((1,), (1,)), ((), ()))
@@ -109,38 +110,26 @@
         )
         relative = jnp.sum(relative.astype(jnp.float32), axis=1, keepdims=True)
         relative = relative.astype(jnp.int32)
-        spot = lax.broadcasted_iota(jnp.int32, (3 * count, 1), 0) + count
-        if kind == "mixed":
-            half = count // 2
-            near = jnp.where(north, 3 * half, 0)
-            far = jnp.where(north, 0, 3 * half)
-            back = relative - 2 * count
-            first = jnp.where(north, 0, 3 * half)
-            last = jnp.where(north, 3 * half, 0) - half
+        half = count // 2
+        roles = [1 + LEGS[kind].index(role) for role in ("north", "south", "shared")]
+        place = relative
+        spot = lax.broadcasted_iota(jnp.int32, (3 * count, 1), 0)
+        partner = jnp.zeros_like(spot)
+        for role, low_half, start_north, start_south in (
+            (roles[0], None, count, count + 3 * half),
+            (roles[1], None, count + 3 * half, count),
+            (roles[2], True, 2 * count, 2 * count + 3 * half),
+            (roles[2], False, 2 * count + 3 * half, 2 * count),
+        ):
+            base = role * count + (0 if low_half in (None, True) else half)
+            extent = count if low_half is None else half
+            start = jnp.where(north, start_north, start_south)
             place = jnp.where(
-                relative < count,
-                relative,
-                jnp.where(
-                    relative < 2 * count,
-                    relative + near,
-                    jnp.where(
-                        relative < 3 * count,
-                        back + 2 * count + jnp.where(back < half, first, last),
-                        relative - 2 * count + far,
-                    ),
-                ),
+                (relative >= base) & (relative < base + extent), relative - base + start, place
             )
-            inside = spot - count
-            second = inside >= 3 * half
-            inside = jnp.where(second, inside - 3 * half, inside)
-            mine = second ^ north
-            spot = jnp.where(
-                inside < count,
-                jnp.where(mine, inside + 3 * count, inside + count),
-                jnp.where(mine, inside + count, inside + count + half),
-            )
-        else:
-            place = relative
+            here = spot + count - start
+            partner = jnp.where((here >= 0) & (here < extent), here + base, partner)
+        spot = partner
         outs.pop(0)[...] = onehot(place, 4 * count)
         kept = jnp.where(spot - 2 * count == beside, 1.0, 0.0)
         kept = jnp.max(kept, axis=1, keepdims=True)
@@ -268,7 +257,7 @@
 
     phases = []
     for begin, end in phase_spans(size_gx, size_gy):
-        kind = "mixed" if end <= size_gy.bit_length() - 1 else "plain"
+        kind = "gy" if end <= size_gy.bit_length() - 1 else "gx"
         phases.append((begin, kind if end - begin > 1 else "single"))
 
     sets = gather_rows(embeddings, device_local_selections)
@@ -283,17 +272,13 @@
             others = [swap(sets, near)]
         else:
             penalty = plan.pop(0)
-            if kind == "mixed":
-                half = count // 2
-                part = jnp.where(north, sets[:half], sets[half:])
-                first = swap(sets, near | high, near)
-                second = swap(part, high)
-                here = jnp.concatenate([first, second], 0)
-                others = [here, swap(here, 1)]
-            else:
-                others = [swap(sets, near)]
-                others.append(swap(sets, high))
-                others.append(swap(sets, near | high))
+            masks = dict(zip(LEGS[kind], (near, high, near | high)))
+            half = count // 2
+            part = jnp.where(north, sets[:half], sets[half:])
+            first = swap(sets, masks["north"], masks["south"])
+            second = swap(part, masks["shared"])
+            here = jnp.concatenate([first, second], 0)
+            others = [here, swap(here, 1)]
         if pending is not None:
             if cover is None:
                 cover, squares = score(embeddings, *pending)

time: 53.9 us -> 57.4 us (1.065)
  starting transfers between devices: 13.7 us -> 15.9 us
  waiting for transfers between devices: 14.5 us -> 15.7 us
    ppermute x12, starting transfers between devices: 13.7 us -> 15.9 us  [swap(): return lax.ppermute(value, ('gx', 'gy'), pairs)]
    ppermute x12, waiting for transfers between devices: 14.5 us -> 15.7 us  [swap(): return lax.ppermute(value, ('gx', 'gy'), pairs)]
    unnamed x8 -> x9, local copies, waits for them, and re-layouts: 8.58 us -> 8.58 us
  transfers between devices with their start and end apart: 12 -> 12, of which waited for: 8 -> 10; matrix products, arithmetic and copies ran while one was open for 3% -> 3% of each run, Pallas kernels for 14% -> 14%
where the time goes in v3:
time: 57.4 us; the launch traced here: 57 us
  starting transfers between devices  15.9 us (28%)
  waiting for transfers between devices  15.7 us (27%)
  Pallas kernels  14.3 us (25%)
  local copies, waits for them, and re-layouts  9.11 us (16%)
  matrix products  1.25 us (2%)
  between operations  0.75 us (1%)
    ppermute x12, starting transfers between devices, swap(): return lax.ppermute(value, ('gx', 'gy'), pairs)  15.9 us
    ppermute x12, waiting for transfers between devices, swap(): return lax.ppermute(value, ('gx', 'gy'), pairs)  15.7 us
    pallas_call x3, Pallas kernels, score(): pl.pallas_call(functools.partial(score_kernel, len(sets), masked, first,...  11.1 us
    unnamed x9, local copies, waits for them, and re-layouts  8.58 us
    pallas_call x1, Pallas kernels, gather_rows(): pl.pallas_call(gather_kernel, out_shape=pltpu.VMEM((count, width), points...  2.97 us
    dot_general x3, matrix products, choose(): jnp.dot(onehot, rows, preferred_element_type=jnp.float32).astype(rows.dtype)  1.25 us
  transfers between devices with their start and end apart: 12, of which 10 were waited for; matrix products, arithmetic and copies ran while one was open for 3% of the time, Pallas kernels for 14%

profile of v3, /device:TPU:0, one launch (start us, length us, event | category | flops | bytes accessed | tf_op | source)
XLA Modules:
  0.0 57.0 jit_solution(11049268309680425537)
XLA Ops:
  0.6 0.0 copy-start.2
  0.6 3.0 %gather_rows.1.refs_0_ = bf16[64,1024]{1,0:T(8,128)(2,1)S(1)} custom-call(s32[1,64]{1,0:T(1,128)} %picks_ref.2, bf16[5120,1024]{1,0:T(8,128)(2,1)} %held_ref.5), custom_call_target="tpu_custom_call" | custom-call | flops 1000000000 | bytes 1048576 | tf_op jit(solution)/shard_map/gather_rows/pallas_call | solution.py:55
  3.6 0.6 collective-permute-start
  4.2 0.0 copy-done.2
  4.2 0.3 plan.1
  4.5 0.7 %collective-permute-done.refs_1_ = bf16[64,1024]{1,0:T(8,128)(2,1)S(1)} collective-permute-done((bf16[64,1024]{1,0:T(8,128)(2,1)S(1)}, bf16[64,1024]{1,0:T(8,128)(2,1)S(1)}, u32[]{:S(2)}, u32[]{:S(2)}) %collective-permute-start) | collective-permute-done | bytes 131104 | tf_op jit(solution)/shard_map/ppermute | solution.py:256
  5.2 0.2 fusion.2
  5.3 5.0 %collective-permute-start.1 = (bf16[64,1024]{1,0:T(8,128)(2,1)S(1)}, bf16[64,1024]{1,0:T(8,128)(2,1)S(1)}, u32[]{:S(2)}, u32[]{:S(2)}) collective-permute-start(bf16[64,1024]{1,0:T(8,128)(2,1)S(1)} %fusion.2), channel_id=1, source_target_pairs={{0,6},{1,5},{2,4},{3,7},{4,2},{5,1},{6,0},{7,3},{8,14},{9,13},{10,... | collective-permute-start | bytes 393224 | tf_op jit(solution)/shard_map/ppermute | solution.py:256
  10.4 0.1 collective-permute-start.2
  10.5 4.3 %collective-permute-done.1 = bf16[64,1024]{1,0:T(8,128)(2,1)S(1)} collective-permute-done((bf16[64,1024]{1,0:T(8,128)(2,1)S(1)}, bf16[64,1024]{1,0:T(8,128)(2,1)S(1)}, u32[]{:S(2)}, u32[]{:S(2)}) %collective-permute-start.1) | collective-permute-done | bytes 131104 | tf_op jit(solution)/shard_map/ppermute | solution.py:256
  14.8 0.6 %collective-permute-done.2 = bf16[32,1024]{1,0:T(8,128)(2,1)S(1)} collective-permute-done((bf16[32,1024]{1,0:T(8,128)(2,1)S(1)}, bf16[32,1024]{1,0:T(8,128)(2,1)S(1)}, u32[]{:S(2)}, u32[]{:S(2)}) %collective-permute-start.2) | collective-permute-done | bytes 65568 | tf_op jit(solution)/shard_map/ppermute | solution.py:256
  15.4 0.0 collective-permute-start.3
  15.4 0.0 copy-start
  15.4 4.0 %copy-done = bf16[5120,1024]{1,0:T(8,128)(2,1)S(1)} copy-done((bf16[5120,1024]{1,0:T(8,128)(2,1)S(1)}, bf16[5120,1024]{1,0:T(8,128)(2,1)}, u32[]{:S(2)}) %copy-start) | copy-done | bytes 10485784
  19.4 3.9 %score_first.1 = (f32[1,5120]{1,0:T(1,128)S(1)}, f32[1,5120]{1,0:T(1,128)S(1)}) custom-call(bf16[5120,1024]{1,0:T(8,128)(2,1)S(1)} %copy-done, bf16[64,1024]{1,0:T(8,128)(2,1)S(1)} %gather_rows.1.refs_0_, bf16[64,1024]{1,0:T(8,128)(2,1)S(1)} %collective-permute-done.refs_1_), custom_call_target="tpu_custom_call" | custom-call | flops 3000000000 | bytes 1048576 | tf_op jit(solution)/shard_map/score_first/pallas_call | solution.py:219
  23.3 0.0 collective-permute-done.3.refs_1_
  23.3 0.2 fusion
  23.5 1.7 %collective-permute-start.4 = (bf16[64,1024]{1,0:T(8,128)(2,1)S(1)}, bf16[64,1024]{1,0:T(8,128)(2,1)S(1)}, u32[]{:S(2)}, u32[]{:S(2)}) collective-permute-start(bf16[64,1024]{1,0:T(8,128)(2,1)S(1)} %fusion), channel_id=1, source_target_pairs={{0,8},{1,25},{2,10},{3,27},{4,12},{5,29},{6,14},{7,31},{8,0},{9,17... | collective-permute-start | bytes 393224 | tf_op jit(solution)/shard_map/ppermute | solution.py:256
  25.2 1.6 %collective-permute-start.5 = (bf16[32,1024]{1,0:T(8,128)(2,1)S(1)}, bf16[32,1024]{1,0:T(8,128)(2,1)S(1)}, u32[]{:S(2)}, u32[]{:S(2)}) collective-permute-start(bf16[32,1024]{1,0:T(8,128)(2,1)S(1)} %slice_select_fusion), channel_id=1, source_target_pairs={{0,16},{1,17},{2,18},{3,19},{4,20},{5,21},{6,22},{7,23},{8,24},{9,... | collective-permute-start | bytes 196616 | tf_op jit(solution)/shard_map/ppermute | solution.py:256
  26.7 2.6 %collective-permute-done.4 = bf16[64,1024]{1,0:T(8,128)(2,1)S(1)} collective-permute-done((bf16[64,1024]{1,0:T(8,128)(2,1)S(1)}, bf16[64,1024]{1,0:T(8,128)(2,1)S(1)}, u32[]{:S(2)}, u32[]{:S(2)}) %collective-permute-start.4) | collective-permute-done | bytes 131104 | tf_op jit(solution)/shard_map/ppermute | solution.py:256
  29.3 1.2 %collective-permute-done.5 = bf16[32,1024]{1,0:T(8,128)(2,1)S(1)} collective-permute-done((bf16[32,1024]{1,0:T(8,128)(2,1)S(1)}, bf16[32,1024]{1,0:T(8,128)(2,1)S(1)}, u32[]{:S(2)}, u32[]{:S(2)}) %collective-permute-start.5) | collective-permute-done | bytes 65568 | tf_op jit(solution)/shard_map/ppermute | solution.py:256
  30.6 0.1 collective-permute-start.6
  30.7 0.0 copy-start.1
  30.7 4.0 %copy-done.1 = bf16[5120,1024]{1,0:T(8,128)(2,1)S(1)} copy-done((bf16[5120,1024]{1,0:T(8,128)(2,1)S(1)}, bf16[5120,1024]{1,0:T(8,128)(2,1)}, u32[]{:S(2)}) %copy-start.1) | copy-done | bytes 10485784
  34.6 3.6 %score.1.refs_3_ = f32[1,5120]{1,0:T(1,128)S(1)} custom-call(bf16[5120,1024]{1,0:T(8,128)(2,1)S(1)} %copy-done.1, bf16[96,1024]{1,0:T(8,128)(2,1)S(1)} %constant_dynamic-update-slice_fusion.refs_0_, bf16[96,1024]{1,0:T(8,128)(2,1)S(1)} %collective-permute-done.3.refs_1_, f32[192,1]{1,0:T(8,128)S(1)} %get-tuple-element.16.refs_2_, ...), custom_call_target="tpu_custom_call" | custom-call | flops 3000000000 | bytes 1048576 | tf_op jit(solution)/shard_map/score/pallas_call | solution.py:219
  38.2 0.0 collective-permute-done.6.refs_1_
  38.2 3.6 %score_last.1 = (f32[1,5120]{1,0:T(1,128)S(1)}, f32[8,128]{1,0:T(8,128)S(1)}) custom-call(bf16[5120,1024]{1,0:T(8,128)(2,1)S(1)} %copy-done.1, bf16[96,1024]{1,0:T(8,128)(2,1)S(1)} %constant_dynamic-update-slice_fusion.2.refs_0_, bf16[96,1024]{1,0:T(8,128)(2,1)S(1)} %collective-permute-done.6.refs_1_, f32[192,1]{1,0:T(8,128)S(1)} %get-tuple-element.15.refs_2_, ...), custom_call_target="tpu_custom_call" | custom-call | flops 3000000000 | bytes 1048576 | tf_op jit(solution)/shard_map/score_last/pallas_call | solution.py:219
  41.9 0.4 collective-permute-start.7
  42.2 0.8 %collective-permute-done.7 = f32[8,128]{1,0:T(8,128)S(1)} collective-permute-done((f32[8,128]{1,0:T(8,128)S(1)}, f32[8,128]{1,0:T(8,128)S(1)}, u32[]{:S(2)}, u32[]{:S(2)}) %collective-permute-start.7) | collective-permute-done | bytes 4128 | tf_op jit(solution)/shard_map/ppermute | solution.py:256
  43.1 1.3 %collective-permute-start.8 = (f32[8,128]{1,0:T(8,128)S(1)}, f32[8,128]{1,0:T(8,128)S(1)}, u32[]{:S(2)}, u32[]{:S(2)}) collective-permute-start(f32[8,128]{1,0:T(8,128)S(1)} %max.15), channel_id=1, source_target_pairs={{0,3},{1,2},{2,1},{3,0},{4,7},{5,6},{6,5},{7,4},{8,11},{9,10},{10,... | collective-permute-start | bytes 12296 | tf_op jit(solution)/shard_map/ppermute | solution.py:256
  44.3 1.8 %collective-permute-done.8 = f32[8,128]{1,0:T(8,128)S(1)} collective-permute-done((f32[8,128]{1,0:T(8,128)S(1)}, f32[8,128]{1,0:T(8,128)S(1)}, u32[]{:S(2)}, u32[]{:S(2)}) %collective-permute-start.8) | collective-permute-done | bytes 4128 | tf_op jit(solution)/shard_map/ppermute | solution.py:256
  46.1 3.0 %collective-permute-start.9 = (f32[8,128]{1,0:T(8,128)S(1)}, f32[8,128]{1,0:T(8,128)S(1)}, u32[]{:S(2)}, u32[]{:S(2)}) collective-permute-start(f32[8,128]{1,0:T(8,128)S(1)} %max.16), channel_id=1, source_target_pairs={{0,5},{1,4},{2,7},{3,6},{4,1},{5,0},{6,3},{7,2},{8,13},{9,12},{10,... | collective-permute-start | bytes 12296 | tf_op jit(solution)/shard_map/ppermute | solution.py:256
  49.1 1.3 %collective-permute-done.9 = f32[8,128]{1,0:T(8,128)S(1)} collective-permute-done((f32[8,128]{1,0:T(8,128)S(1)}, f32[8,128]{1,0:T(8,128)S(1)}, u32[]{:S(2)}, u32[]{:S(2)}) %collective-permute-start.9) | collective-permute-done | bytes 4128 | tf_op jit(solution)/shard_map/ppermute | solution.py:256
  50.5 1.0 %collective-permute-start.10 = (f32[8,128]{1,0:T(8,128)S(1)}, f32[8,128]{1,0:T(8,128)S(1)}, u32[]{:S(2)}, u32[]{:S(2)}) collective-permute-start(f32[8,128]{1,0:T(8,128)S(1)} %max.17), channel_id=1, source_target_pairs={{0,9},{1,8},{2,11},{3,10},{4,13},{5,12},{6,15},{7,14},{8,1},{9,0},... | collective-permute-start | bytes 12296 | tf_op jit(solution)/shard_map/ppermute | solution.py:256
  51.5 2.0 %collective-permute-done.10 = f32[8,128]{1,0:T(8,128)S(1)} collective-permute-done((f32[8,128]{1,0:T(8,128)S(1)}, f32[8,128]{1,0:T(8,128)S(1)}, u32[]{:S(2)}, u32[]{:S(2)}) %collective-permute-start.10) | collective-permute-done | bytes 4128 | tf_op jit(solution)/shard_map/ppermute | solution.py:256
  53.5 1.2 %collective-permute-start.11 = (f32[8,128]{1,0:T(8,128)S(1)}, f32[8,128]{1,0:T(8,128)S(1)}, u32[]{:S(2)}, u32[]{:S(2)}) collective-permute-start(f32[8,128]{1,0:T(8,128)S(1)} %max.18), channel_id=1, source_target_pairs={{0,17},{1,16},{2,19},{3,18},{4,21},{5,20},{6,23},{7,22},{8,25},{9,... | collective-permute-start | bytes 12296 | tf_op jit(solution)/shard_map/ppermute | solution.py:256
  54.7 0.9 %fusion.1 = bf16[64,1024]{1,0:T(8,128)(2,1)} fusion(bf16[64,256]{1,0:T(8,128)(2,1)S(1)} %get-tuple-element.14, bf16[96,1024]{1,0:T(8,128)(2,1)S(1)} %collective-permute-done.6.refs_1_, bf16[32,1024]{1,0:T(8,128)(2,1)S(1)} %collective-permute-done.5, bf16[64,1024]{1,0:T(8,128)(2,1)S(1)} %collective-permute-done.4, bf16[64,1024]{1,0:T(8,128)(2,1)S(1)} %fusion), kind=kOutput, calls=%fused_computation.4 | convolution fusion | flops 35717120 | bytes 688128 | tf_op jit(solution)/shard_map/dot_general | solution.py:232
  55.6 0.6 %copy.8 = f32[5120]{0:T(1024)} copy(f32[5120]{0:T(1024)S(1)} %bitcast.11) | data formatting | bytes 40960
  56.2 0.3 collective-permute-done.11
  56.5 0.5 slice.19
  (11 shorter events, 0.1 us)
Async XLA Ops:
  0.6 3.6 %copy-start.2 = (s32[32,64]{1,0:T(8,128)S(1)}, s32[32,64]{1,0:T(8,128)}, u32[]{:S(2)}) copy-start(s32[32,64]{1,0:T(8,128)} %picks_ref.3) | copy-start | bytes 24580
  3.6 1.5 %collective-permute-start = (bf16[64,1024]{1,0:T(8,128)(2,1)S(1)}, bf16[64,1024]{1,0:T(8,128)(2,1)S(1)}, u32[]{:S(2)}, u32[]{:S(2)}) collective-permute-start(bf16[64,1024]{1,0:T(8,128)(2,1)S(1)} %gather_rows.1.refs_0_), channel_id=1, source_target_pairs={{0,1},{1,0},{2,3},{3,2},{4,5},{5,4},{6,7},{7,6},{8,9},{9,8},{10,11... | collective-permute-start | bytes 393224 | tf_op jit(solution)/shard_map/ppermute | solution.py:256
  5.3 9.4 %collective-permute-start.1 = (bf16[64,1024]{1,0:T(8,128)(2,1)S(1)}, bf16[64,1024]{1,0:T(8,128)(2,1)S(1)}, u32[]{:S(2)}, u32[]{:S(2)}) collective-permute-start(bf16[64,1024]{1,0:T(8,128)(2,1)S(1)} %fusion.2), channel_id=1, source_target_pairs={{0,6},{1,5},{2,4},{3,7},{4,2},{5,1},{6,0},{7,3},{8,14},{9,13},{10,... | collective-permute-start | bytes 393224 | tf_op jit(solution)/shard_map/ppermute | solution.py:256
  10.4 5.0 %collective-permute-start.2 = (bf16[32,1024]{1,0:T(8,128)(2,1)S(1)}, bf16[32,1024]{1,0:T(8,128)(2,1)S(1)}, u32[]{:S(2)}, u32[]{:S(2)}) collective-permute-start(bf16[32,1024]{1,0:T(8,128)(2,1)S(1)} %slice_select_fusion.1), channel_id=1, source_target_pairs={{0,2},{1,3},{2,0},{3,1},{4,6},{5,7},{6,4},{7,5},{8,10},{9,11},{10,... | collective-permute-start | bytes 196616 | tf_op jit(solution)/shard_map/ppermute | solution.py:256
  15.4 7.9 %collective-permute-start.3 = (bf16[96,1024]{1,0:T(8,128)(2,1)S(1)}, bf16[96,1024]{1,0:T(8,128)(2,1)S(1)}, u32[]{:S(2)}, u32[]{:S(2)}) collective-permute-start(bf16[96,1024]{1,0:T(8,128)(2,1)S(1)} %constant_dynamic-update-slice_fusion.refs_0_), channel_id=1, source_target_pairs={{0,1},{1,0},{2,3},{3,2},{4,5},{5,4},{6,7},{7,6},{8,9},{9,8},{10,11... | collective-permute-start | bytes 589832 | tf_op jit(solution)/shard_map/ppermute | solution.py:256
  15.4 4.0 %copy-start = (bf16[5120,1024]{1,0:T(8,128)(2,1)S(1)}, bf16[5120,1024]{1,0:T(8,128)(2,1)}, u32[]{:S(2)}) copy-start(bf16[5120,1024]{1,0:T(8,128)(2,1)} %held_ref.5) | copy-start | bytes 31457284
  23.5 5.8 %collective-permute-start.4 = (bf16[64,1024]{1,0:T(8,128)(2,1)S(1)}, bf16[64,1024]{1,0:T(8,128)(2,1)S(1)}, u32[]{:S(2)}, u32[]{:S(2)}) collective-permute-start(bf16[64,1024]{1,0:T(8,128)(2,1)S(1)} %fusion), channel_id=1, source_target_pairs={{0,8},{1,25},{2,10},{3,27},{4,12},{5,29},{6,14},{7,31},{8,0},{9,17... | collective-permute-start | bytes 393224 | tf_op jit(solution)/shard_map/ppermute | solution.py:256
  25.2 5.4 %collective-permute-start.5 = (bf16[32,1024]{1,0:T(8,128)(2,1)S(1)}, bf16[32,1024]{1,0:T(8,128)(2,1)S(1)}, u32[]{:S(2)}, u32[]{:S(2)}) collective-permute-start(bf16[32,1024]{1,0:T(8,128)(2,1)S(1)} %slice_select_fusion), channel_id=1, source_target_pairs={{0,16},{1,17},{2,18},{3,19},{4,20},{5,21},{6,22},{7,23},{8,24},{9,... | collective-permute-start | bytes 196616 | tf_op jit(solution)/shard_map/ppermute | solution.py:256
  30.6 7.7 %collective-permute-start.6 = (bf16[96,1024]{1,0:T(8,128)(2,1)S(1)}, bf16[96,1024]{1,0:T(8,128)(2,1)S(1)}, u32[]{:S(2)}, u32[]{:S(2)}) collective-permute-start(bf16[96,1024]{1,0:T(8,128)(2,1)S(1)} %constant_dynamic-update-slice_fusion.2.refs_0_), channel_id=1, source_target_pairs={{0,1},{1,0},{2,3},{3,2},{4,5},{5,4},{6,7},{7,6},{8,9},{9,8},{10,11... | collective-permute-start | bytes 589832 | tf_op jit(solution)/shard_map/ppermute | solution.py:256
  30.7 4.0 %copy-start.1 = (bf16[5120,1024]{1,0:T(8,128)(2,1)S(1)}, bf16[5120,1024]{1,0:T(8,128)(2,1)}, u32[]{:S(2)}) copy-start(bf16[5120,1024]{1,0:T(8,128)(2,1)} %held_ref.5) | copy-start | bytes 31457284
  41.9 1.2 %collective-permute-start.7 = (f32[8,128]{1,0:T(8,128)S(1)}, f32[8,128]{1,0:T(8,128)S(1)}, u32[]{:S(2)}, u32[]{:S(2)}) collective-permute-start(f32[8,128]{1,0:T(8,128)S(1)} %get-tuple-element.20), channel_id=1, source_target_pairs={{0,1},{1,0},{2,3},{3,2},{4,5},{5,4},{6,7},{7,6},{8,9},{9,8},{10,11... | collective-permute-start | bytes 12296 | tf_op jit(solution)/shard_map/ppermute | solution.py:256
  43.1 3.0 %collective-permute-start.8 = (f32[8,128]{1,0:T(8,128)S(1)}, f32[8,128]{1,0:T(8,128)S(1)}, u32[]{:S(2)}, u32[]{:S(2)}) collective-permute-start(f32[8,128]{1,0:T(8,128)S(1)} %max.15), channel_id=1, source_target_pairs={{0,3},{1,2},{2,1},{3,0},{4,7},{5,6},{6,5},{7,4},{8,11},{9,10},{10,... | collective-permute-start | bytes 12296 | tf_op jit(solution)/shard_map/ppermute | solution.py:256
  46.1 4.3 %collective-permute-start.9 = (f32[8,128]{1,0:T(8,128)S(1)}, f32[8,128]{1,0:T(8,128)S(1)}, u32[]{:S(2)}, u32[]{:S(2)}) collective-permute-start(f32[8,128]{1,0:T(8,128)S(1)} %max.16), channel_id=1, source_target_pairs={{0,5},{1,4},{2,7},{3,6},{4,1},{5,0},{6,3},{7,2},{8,13},{9,12},{10,... | collective-permute-start | bytes 12296 | tf_op jit(solution)/shard_map/ppermute | solution.py:256
  50.5 3.0 %collective-permute-start.10 = (f32[8,128]{1,0:T(8,128)S(1)}, f32[8,128]{1,0:T(8,128)S(1)}, u32[]{:S(2)}, u32[]{:S(2)}) collective-permute-start(f32[8,128]{1,0:T(8,128)S(1)} %max.17), channel_id=1, source_target_pairs={{0,9},{1,8},{2,11},{3,10},{4,13},{5,12},{6,15},{7,14},{8,1},{9,0},... | collective-permute-start | bytes 12296 | tf_op jit(solution)/shard_map/ppermute | solution.py:256
  53.5 3.0 %collective-permute-start.11 = (f32[8,128]{1,0:T(8,128)S(1)}, f32[8,128]{1,0:T(8,128)S(1)}, u32[]{:S(2)}, u32[]{:S(2)}) collective-permute-start(f32[8,128]{1,0:T(8,128)S(1)} %max.18), channel_id=1, source_target_pairs={{0,17},{1,16},{2,19},{3,18},{4,21},{5,20},{6,23},{7,22},{8,25},{9,... | collective-permute-start | bytes 12296 | tf_op jit(solution)/shard_map/ppermute | solution.py:256

commit v4 on v3

v4 whole, which is shorter than its diff:
```python
import functools

import jax
import jax.numpy as jnp
from jax import lax
from jax.experimental import pallas as pl
from jax.experimental.pallas import tpu as pltpu
from jax.sharding import PartitionSpec as P


GROUP = 8
LEGS = {"gy": ("shared", "north", "south"), "gx": ("south", "shared", "north")}
CHUNK = 256
NT = (((1,), (1,)), ((), ()))
VMEM = pl.BlockSpec(memory_space=pltpu.VMEM)


def cost(flops):
    return pl.CostEstimate(flops=flops, bytes_accessed=2**20, transcendentals=0)


def gather_kernel(picks_ref, points_ref, out_ref, held, sem):
    count = out_ref.shape[0]
    picks = [picks_ref[0, i] for i in range(count)]
    for i, pick in enumerate(picks):
        start = pl.multiple_of(lax.shift_right_logical(pick, 3) * GROUP, GROUP)
        pltpu.make_async_copy(
            points_ref.at[pl.ds(start, GROUP), :], held.at[pl.ds(i * GROUP, GROUP), :], sem
        ).start()
    down = lax.broadcasted_iota(jnp.int32, (count, 128), 0)
    wanted = down * GROUP
    for i, pick in enumerate(picks):
        wanted = jnp.where(down == i, wanted + (pick & (GROUP - 1)), wanted)
    lanes = lax.broadcasted_iota(jnp.int32, (count, 128), 1)
    onehot = jnp.concatenate(
        [(lanes + base == wanted).astype(jnp.bfloat16) for base in range(0, count * GROUP, 128)],
        axis=1,
    )
    pltpu.make_async_copy(points_ref.at[pl.ds(0, count * GROUP), :], held, sem).wait()
    out_ref[...] = jnp.dot(
        onehot, held[...], preferred_element_type=jnp.float32
    ).astype(jnp.bfloat16)


def gather_rows(points, picks):
    count = picks.shape[1]
    width = points.shape[1]
    return pl.pallas_call(
        gather_kernel,
        out_shape=pltpu.VMEM((count, width), points.dtype),
        in_specs=[
            pl.BlockSpec(memory_space=pltpu.SMEM),
            pl.BlockSpec(memory_space=pltpu.HBM),
        ],
        out_specs=VMEM,
        scratch_shapes=[
            pltpu.VMEM((count * GROUP, width), points.dtype),
            pltpu.SemaphoreType.DMA,
        ],
        compiler_params=pltpu.CompilerParams(vmem_limit_bytes=56 * 2**20),
        cost_estimate=cost(10**9),
        name="gather_rows",
    )(picks, points)


def swap_halves(index, count, lower):
    swapped_index = jnp.where(index < count, index + count, index - count)
    return jnp.where(lower, index, swapped_index)


def upright(row):
    size = row.shape[1]
    across = lax.broadcasted_iota(jnp.int32, (size, size), 1)
    down = lax.broadcasted_iota(jnp.int32, (size, size), 0)
    spread = jnp.where(across == down, jnp.broadcast_to(row, (size, size)), 0)
    return jnp.sum(spread.astype(jnp.float32), axis=1, keepdims=True).astype(jnp.int32)


def plan_kernel(phases, count, devices, picks_ref, *out_refs):
    number = lax.axis_index("gx") * lax.axis_size("gy") + lax.axis_index("gy")
    outs = list(out_refs)
    north = (number & 1) == 1

    def row_of(step, place):
        return picks_ref[pl.ds(devices - (devices >> step) + (place >> step + 1), 1), :]

    def onehot(column, total):
        lanes = lax.broadcasted_iota(jnp.int32, (column.shape[0], total), 1)
        return (lanes == column).astype(jnp.bfloat16)

    for step, kind in phases:
        lower = (number >> step & 1) == 0
        own = swap_halves(row_of(step, number), count, lower)
        if kind == "single":
            outs.pop(0)[...] = onehot(upright(own), 2 * count)
            continue
        beside = swap_halves(row_of(step, number ^ 2 << step), count, lower)
        lower_next = (number >> step + 1 & 1) == 0
        top = upright(swap_halves(row_of(step + 1, number), count, lower_next))
        lanes = lax.broadcasted_iota(jnp.int32, (count, count), 1)
        relative = jnp.where(lanes == top, own, 0) + jnp.where(
            lanes + count == top, beside + 2 * count, 0
        )
        relative = jnp.sum(relative.astype(jnp.float32), axis=1, keepdims=True)
        relative = relative.astype(jnp.int32)
        half = count // 2
        roles = [1 + LEGS[kind].index(role) for role in ("north", "south", "shared")]

        def placed(relative):
            place = relative
            for role, part, start_north, start_south in (
                (roles[0], None, count, count + 3 * half),
                (roles[1], None, count + 3 * half, count),
                (roles[2], 0, 2 * count, 2 * count + 3 * half),
                (roles[2], 1, 2 * count + 3 * half, 2 * count),
            ):
                base = role * count + (part or 0) * half
                extent = count if part is None else half
                inside = (relative >= base) & (relative < base + extent)
                start = jnp.where(north, start_north, start_south)
                place = jnp.where(inside, relative - base + start, place)
            return place

        outs.pop(0)[...] = onehot(placed(relative), 4 * count)
        plain = lax.broadcasted_iota(jnp.int32, (count, 1), 0) + count
        scored = jnp.concatenate([plain, upright(beside) + 2 * count], 0)
        outs.pop(0)[...] = onehot(placed(scored) - count, 3 * count)


def make_plan(picks, phases, devices):
    count = picks.shape[1]
    shapes = []
    for _, kind in phases:
        if kind == "single":
            shapes.append(pltpu.VMEM((count, 2 * count), jnp.bfloat16))
        else:
            shapes.append(pltpu.VMEM((count, 4 * count), jnp.bfloat16))
            shapes.append(pltpu.VMEM((2 * count, 3 * count), jnp.bfloat16))
    return pl.pallas_call(
        functools.partial(plan_kernel, phases, count, devices),
        out_shape=tuple(shapes),
        in_specs=[VMEM],
        out_specs=(VMEM,) * len(shapes),
        compiler_params=pltpu.CompilerParams(vmem_limit_bytes=4 * 2**20),
        cost_estimate=pl.CostEstimate(flops=10**10, bytes_accessed=2**27, transcendentals=0),
        name="plan",
    )(picks)


def prepare_kernel(points_ref, turned_ref, squares_ref):
    rows, width = points_ref.shape
    ones = jnp.ones((8, 128), jnp.bfloat16)
    down = lax.broadcasted_iota(jnp.int32, (CHUNK, CHUNK), 0)
    across = lax.broadcasted_iota(jnp.int32, (CHUNK, CHUNK), 1)
    identity = (down == across).astype(jnp.bfloat16)
    for piece in range(rows // CHUNK):
        window = pl.ds(piece * CHUNK, CHUNK)
        partial = None
        for lane in range(0, width, CHUNK):
            value = points_ref[window, pl.ds(lane, CHUNK)]
            turned_ref[pl.ds(lane, CHUNK), window] = lax.dot_general(
                identity, value, NT, preferred_element_type=jnp.float32
            ).astype(jnp.bfloat16)
            block = value.astype(jnp.float32)
            block = block * block
            for offset in range(0, CHUNK, 128):
                term = block[:, offset : offset + 128]
                partial = term if partial is None else partial + term
        high = partial.astype(jnp.bfloat16)
        low = (partial - high.astype(jnp.float32)).astype(jnp.bfloat16)
        total = lax.dot_general(
            ones, high, NT, preferred_element_type=jnp.float32
        ) + lax.dot_general(ones, low, NT, preferred_element_type=jnp.float32)
        squares_ref[:, window] = total[:1, :]


def prepare(points):
    rows, width = points.shape
    return pl.pallas_call(
        prepare_kernel,
        out_shape=(
            pltpu.VMEM((width, rows), points.dtype),
            pltpu.VMEM((1, rows), jnp.float32),
        ),
        in_specs=[VMEM],
        out_specs=(VMEM, VMEM),
        compiler_params=pltpu.CompilerParams(vmem_limit_bytes=16 * 2**20),
        cost_estimate=cost(3 * 10**9),
        name="prepare",
    )(points)


def score_kernel(shape, first, last, turned_ref, *refs):
    width, rows = turned_ref.shape
    refs = list(refs)
    values = []
    for chosen, number in shape:
        onehot = refs.pop(0)[...] if chosen else None
        value = jnp.concatenate([refs.pop(0)[...] for _ in range(number)], 0)
        if chosen:
            value = jnp.dot(onehot, value, preferred_element_type=jnp.float32)
            value = value.astype(jnp.bfloat16)
        values.append(value)
    value = values[0] if len(values) == 1 else jnp.concatenate(values, 0)
    wide = value.astype(jnp.float32)
    top = jnp.sum(wide * wide, axis=1, keepdims=True)
    weight = value * jnp.bfloat16(-2.0)
    before_ref = None if first else refs.pop(0)
    squares_ref = refs.pop(0) if last else None
    out_ref = refs.pop(0)
    peak = None
    for piece in range(rows // CHUNK):
        window = pl.ds(piece * CHUNK, CHUNK)
        part = jnp.dot(weight, turned_ref[:, window], preferred_element_type=jnp.float32)
        least = jnp.min(part + top, axis=0, keepdims=True)
        if not first:
            least = jnp.minimum(least, before_ref[:, window])
        if last:
            least = (least + squares_ref[:, window]) / width
            peak = least if peak is None else jnp.maximum(peak, least)
        out_ref[:, window] = least
    if last:
        rest = refs.pop(0)
        rest[...] = jnp.broadcast_to(jnp.max(peak, axis=1, keepdims=True), rest.shape)


def score(turned, pending, before=None, squares=None, last=False):
    rows = turned.shape[1]
    operands = [turned]
    shape = []
    for onehot, sets in pending:
        shape.append((onehot is not None, len(sets)))
        operands += ([] if onehot is None else [onehot]) + list(sets)
    if before is not None:
        operands.append(before)
    if last:
        operands.append(squares)
    out_shape = [pltpu.VMEM((1, rows), jnp.float32)]
    if last:
        out_shape.append(pltpu.VMEM((8, 128), jnp.float32))
    return pl.pallas_call(
        functools.partial(score_kernel, tuple(shape), before is None, last),
        out_shape=tuple(out_shape),
        in_specs=[VMEM] * len(operands),
        out_specs=(VMEM,) * len(out_shape),
        compiler_params=pltpu.CompilerParams(vmem_limit_bytes=16 * 2**20),
        cost_estimate=cost(3 * 10**9),
        name="score_last" if last else "score",
    )(*operands)


def choose(onehot, held):
    rows = held[0] if len(held) == 1 else jnp.concatenate(held, 0)
    return jnp.dot(onehot, rows, preferred_element_type=jnp.float32).astype(rows.dtype)


def phase_spans(size_gx, size_gy):
    bits_gy = size_gy.bit_length() - 1
    rounds = bits_gy + size_gx.bit_length() - 1
    spans = [(0, 1)]
    for begin, end in ((1, bits_gy), (bits_gy, rounds)):
        for step in range(begin, end, 2):
            spans.append((step, min(step + 2, end)))
    return spans


def per_device(embeddings, device_local_selections, merge_picks):
    count = device_local_selections.shape[1]
    size_gx = lax.axis_size("gx")
    size_gy = lax.axis_size("gy")
    devices = size_gx * size_gy
    number = lax.axis_index("gx") * size_gy + lax.axis_index("gy")
    north = (number & 1) == 1

    def swap(value, mask, other=None):
        other = mask if other is None else other
        pairs = [(source, source ^ (mask if source & 1 else other)) for source in range(devices)]
        return lax.ppermute(value, ("gx", "gy"), pairs)

    phases = []
    for begin, end in phase_spans(size_gx, size_gy):
        kind = "gy" if end <= size_gy.bit_length() - 1 else "gx"
        phases.append((begin, kind if end - begin > 1 else "single"))

    sets = gather_rows(embeddings, device_local_selections)
    plan = list(make_plan(merge_picks, phases, devices))
    cover = None
    pending = []
    for place, (step, kind) in enumerate(phases):
        near, high = 1 << step, 2 << step
        onehot = plan.pop(0)
        if kind == "single":
            kept = None
            others = [swap(sets, near)]
        else:
            kept = plan.pop(0)
            masks = dict(zip(LEGS[kind], (near, high, near | high)))
            half = count // 2
            part = jnp.where(north, sets[:half], sets[half:])
            first = swap(sets, masks["north"], masks["south"])
            second = swap(part, masks["shared"])
            here = jnp.concatenate([first, second], 0)
            others = [here, swap(here, 1)]
        if place == 1:
            turned, squares = prepare(embeddings)
        elif place > 1:
            (cover,) = score(turned, pending, cover)
            pending = []
        pending.append((kept, ([sets] if step == 0 else []) + others))
        sets = choose(onehot, [sets] + others)
    cover, peak = score(turned, pending, cover, squares, last=True)
    bit = 1
    while bit < devices:
        peak = jnp.maximum(peak, swap(peak, bit | 1))
        bit *= 2
    return (sets, cover[0], peak[0, 0])


def solution(mesh):
    return jax.shard_map(
        per_device,
        mesh=mesh,
        in_specs=(P(("gx", "gy"), None), P(("gx", "gy"), None), P()),
        out_specs=(P(), P(("gx", "gy")), P()),
        check_vma=False,
    )
```

time: 57.4 us -> 50.6 us (0.88)
  local copies, waits for them, and re-layouts: 9.11 us -> 5.13 us
  Pallas kernels: 14.3 us -> 11.6 us
    unnamed x9 -> x7, local copies, waits for them, and re-layouts: 8.58 us -> 4.6 us
    pallas_call x3, Pallas kernels: 11.1 us -> 8.99 us  [the longest x2 4.82 us: score(): pl.pallas_call(functools.partial(score_kernel, tuple(shape), before is No...]
    pallas_call x1, Pallas kernels: 2.97 us -> 2.29 us  [gather_rows(): pl.pallas_call(gather_kernel, out_shape=pltpu.VMEM((count, width), points...]
  transfers between devices with their start and end apart: 12 -> 12, of which waited for: 10 -> 10; matrix products, arithmetic and copies ran while one was open for 3% -> 3% of each run, Pallas kernels for 14% -> 15%
where the time goes in v4:
time: 50.6 us; the launch traced here: 50.3 us
  starting transfers between devices  15.9 us (31%)
  waiting for transfers between devices  15.7 us (31%)
  Pallas kernels  11.6 us (23%)
  local copies, waits for them, and re-layouts  5.13 us (10%)
  matrix products  1.25 us (2%)
  between operations  0.76 us (2%)
    ppermute x12, starting transfers between devices, swap(): return lax.ppermute(value, ('gx', 'gy'), pairs)  15.9 us
    ppermute x12, waiting for transfers between devices, swap(): return lax.ppermute(value, ('gx', 'gy'), pairs)  15.7 us
    pallas_call x2, Pallas kernels, score(): pl.pallas_call(functools.partial(score_kernel, tuple(shape), before is No...  4.82 us
    unnamed x7, local copies, waits for them, and re-layouts  4.6 us
    pallas_call x1, Pallas kernels, prepare(): pl.pallas_call(prepare_kernel, out_shape=(pltpu.VMEM((width, rows), point...  4.17 us
    pallas_call x1, Pallas kernels, gather_rows(): pl.pallas_call(gather_kernel, out_shape=pltpu.VMEM((count, width), points...  2.29 us
    dot_general x3, matrix products, choose(): jnp.dot(onehot, rows, preferred_element_type=jnp.float32).astype(rows.dtype)  1.25 us
  transfers between devices with their start and end apart: 12, of which 10 were waited for; matrix products, arithmetic and copies ran while one was open for 3% of the time, Pallas kernels for 15%

profile of v4, /device:TPU:0, one launch (start us, length us, event | category | flops | bytes accessed | tf_op | source)
XLA Modules:
  0.0 50.3 jit_solution(10169786664124346127)
XLA Ops:
  0.6 0.0 copy-start.1
  0.6 2.3 %gather_rows.1.refs_0_ = bf16[64,1024]{1,0:T(8,128)(2,1)S(1)} custom-call(s32[1,64]{1,0:T(1,128)} %picks_ref.2, bf16[5120,1024]{1,0:T(8,128)(2,1)} %points_ref.3), custom_call_target="tpu_custom_call" | custom-call | flops 1000000000 | bytes 1048576 | tf_op jit(solution)/shard_map/gather_rows/pallas_call | solution.py:48
  2.9 0.6 %collective-permute-start = (bf16[64,1024]{1,0:T(8,128)(2,1)S(1)}, bf16[64,1024]{1,0:T(8,128)(2,1)S(1)}, u32[]{:S(2)}, u32[]{:S(2)}) collective-permute-start(bf16[64,1024]{1,0:T(8,128)(2,1)S(1)} %gather_rows.1.refs_0_), channel_id=1, source_target_pairs={{0,1},{1,0},{2,3},{3,2},{4,5},{5,4},{6,7},{7,6},{8,9},{9,8},{10,11... | collective-permute-start | bytes 393224 | tf_op jit(solution)/shard_map/ppermute | solution.py:278
  3.5 0.0 copy-done.1
  3.5 0.3 plan.1
  3.8 0.7 %collective-permute-done.refs_1_ = bf16[64,1024]{1,0:T(8,128)(2,1)S(1)} collective-permute-done((bf16[64,1024]{1,0:T(8,128)(2,1)S(1)}, bf16[64,1024]{1,0:T(8,128)(2,1)S(1)}, u32[]{:S(2)}, u32[]{:S(2)}) %collective-permute-start) | collective-permute-done | bytes 131104 | tf_op jit(solution)/shard_map/ppermute | solution.py:278
  4.5 0.2 fusion.2
  4.7 5.0 %collective-permute-start.1 = (bf16[64,1024]{1,0:T(8,128)(2,1)S(1)}, bf16[64,1024]{1,0:T(8,128)(2,1)S(1)}, u32[]{:S(2)}, u32[]{:S(2)}) collective-permute-start(bf16[64,1024]{1,0:T(8,128)(2,1)S(1)} %fusion.2), channel_id=1, source_target_pairs={{0,6},{1,5},{2,4},{3,7},{4,2},{5,1},{6,0},{7,3},{8,14},{9,13},{10,... | collective-permute-start | bytes 393224 | tf_op jit(solution)/shard_map/ppermute | solution.py:278
  9.7 0.1 collective-permute-start.2
  9.8 4.3 %collective-permute-done.1 = bf16[64,1024]{1,0:T(8,128)(2,1)S(1)} collective-permute-done((bf16[64,1024]{1,0:T(8,128)(2,1)S(1)}, bf16[64,1024]{1,0:T(8,128)(2,1)S(1)}, u32[]{:S(2)}, u32[]{:S(2)}) %collective-permute-start.1) | collective-permute-done | bytes 131104 | tf_op jit(solution)/shard_map/ppermute | solution.py:278
  14.1 0.6 %collective-permute-done.2 = bf16[32,1024]{1,0:T(8,128)(2,1)S(1)} collective-permute-done((bf16[32,1024]{1,0:T(8,128)(2,1)S(1)}, bf16[32,1024]{1,0:T(8,128)(2,1)S(1)}, u32[]{:S(2)}, u32[]{:S(2)}) %collective-permute-start.2) | collective-permute-done | bytes 65568 | tf_op jit(solution)/shard_map/ppermute | solution.py:278
  14.7 0.0 collective-permute-start.3
  14.7 0.0 copy-start
  14.7 4.0 %copy-done = bf16[5120,1024]{1,0:T(8,128)(2,1)S(1)} copy-done((bf16[5120,1024]{1,0:T(8,128)(2,1)S(1)}, bf16[5120,1024]{1,0:T(8,128)(2,1)}, u32[]{:S(2)}) %copy-start) | copy-done | bytes 10485784
  18.7 4.2 %prepare.1 = (bf16[1024,5120]{1,0:T(8,128)(2,1)S(1)}, f32[1,5120]{1,0:T(1,128)S(1)}) custom-call(bf16[5120,1024]{1,0:T(8,128)(2,1)S(1)} %copy-done), custom_call_target="tpu_custom_call" | custom-call | flops 3000000000 | bytes 1048576 | tf_op jit(solution)/shard_map/prepare/pallas_call | solution.py:179
  22.9 0.0 collective-permute-done.3.refs_4_
  22.9 0.2 fusion
  23.1 1.7 %collective-permute-start.4 = (bf16[64,1024]{1,0:T(8,128)(2,1)S(1)}, bf16[64,1024]{1,0:T(8,128)(2,1)S(1)}, u32[]{:S(2)}, u32[]{:S(2)}) collective-permute-start(bf16[64,1024]{1,0:T(8,128)(2,1)S(1)} %fusion), channel_id=1, source_target_pairs={{0,8},{1,25},{2,10},{3,27},{4,12},{5,29},{6,14},{7,31},{8,0},{9,17... | collective-permute-start | bytes 393224 | tf_op jit(solution)/shard_map/ppermute | solution.py:278
  24.8 1.6 %collective-permute-start.5 = (bf16[32,1024]{1,0:T(8,128)(2,1)S(1)}, bf16[32,1024]{1,0:T(8,128)(2,1)S(1)}, u32[]{:S(2)}, u32[]{:S(2)}) collective-permute-start(bf16[32,1024]{1,0:T(8,128)(2,1)S(1)} %slice_select_fusion), channel_id=1, source_target_pairs={{0,16},{1,17},{2,18},{3,19},{4,20},{5,21},{6,22},{7,23},{8,24},{9,... | collective-permute-start | bytes 196616 | tf_op jit(solution)/shard_map/ppermute | solution.py:278
  26.3 2.6 %collective-permute-done.4 = bf16[64,1024]{1,0:T(8,128)(2,1)S(1)} collective-permute-done((bf16[64,1024]{1,0:T(8,128)(2,1)S(1)}, bf16[64,1024]{1,0:T(8,128)(2,1)S(1)}, u32[]{:S(2)}, u32[]{:S(2)}) %collective-permute-start.4) | collective-permute-done | bytes 131104 | tf_op jit(solution)/shard_map/ppermute | solution.py:278
  29.0 1.2 %collective-permute-done.5 = bf16[32,1024]{1,0:T(8,128)(2,1)S(1)} collective-permute-done((bf16[32,1024]{1,0:T(8,128)(2,1)S(1)}, bf16[32,1024]{1,0:T(8,128)(2,1)S(1)}, u32[]{:S(2)}, u32[]{:S(2)}) %collective-permute-start.5) | collective-permute-done | bytes 65568 | tf_op jit(solution)/shard_map/ppermute | solution.py:278
  30.2 0.1 collective-permute-start.6
  30.3 3.0 %score.1.refs_3_ = f32[1,5120]{1,0:T(1,128)S(1)} custom-call(bf16[1024,5120]{1,0:T(8,128)(2,1)S(1)} %get-tuple-element.15.turned_ref, bf16[64,1024]{1,0:T(8,128)(2,1)S(1)} %gather_rows.1.refs_0_, bf16[64,1024]{1,0:T(8,128)(2,1)S(1)} %collective-permute-done.refs_1_, bf16[128,192]{1,0:T(8,128)(2,1)S(1)} %get-tuple-element.17.refs_2_, ...), custom_call_target="tpu_custom_call" | custom-call | flops 3000000000 | bytes 1048576 | tf_op jit(solution)/shard_map/score/pallas_call | solution.py:241
  33.3 0.0 collective-permute-done.6.refs_2_
  33.3 1.8 %score_last.1 = (f32[1,5120]{1,0:T(1,128)S(1)}, f32[8,128]{1,0:T(8,128)S(1)}) custom-call(bf16[1024,5120]{1,0:T(8,128)(2,1)S(1)} %get-tuple-element.15.turned_ref, bf16[128,192]{1,0:T(8,128)(2,1)S(1)} %get-tuple-element.16.refs_0_, bf16[96,1024]{1,0:T(8,128)(2,1)S(1)} %constant_dynamic-update-slice_fusion.2.refs_1_, ...), custom_call_target="tpu_custom_call" | custom-call | flops 3000000000 | bytes 1048576 | tf_op jit(solution)/shard_map/score_last/pallas_call | solution.py:241
  35.1 0.4 collective-permute-start.7
  35.5 0.8 %collective-permute-done.7 = f32[8,128]{1,0:T(8,128)S(1)} collective-permute-done((f32[8,128]{1,0:T(8,128)S(1)}, f32[8,128]{1,0:T(8,128)S(1)}, u32[]{:S(2)}, u32[]{:S(2)}) %collective-permute-start.7) | collective-permute-done | bytes 4128 | tf_op jit(solution)/shard_map/ppermute | solution.py:278
  36.3 1.3 %collective-permute-start.8 = (f32[8,128]{1,0:T(8,128)S(1)}, f32[8,128]{1,0:T(8,128)S(1)}, u32[]{:S(2)}, u32[]{:S(2)}) collective-permute-start(f32[8,128]{1,0:T(8,128)S(1)} %max.15), channel_id=1, source_target_pairs={{0,3},{1,2},{2,1},{3,0},{4,7},{5,6},{6,5},{7,4},{8,11},{9,10},{10,... | collective-permute-start | bytes 12296 | tf_op jit(solution)/shard_map/ppermute | solution.py:278
  37.6 1.8 %collective-permute-done.8 = f32[8,128]{1,0:T(8,128)S(1)} collective-permute-done((f32[8,128]{1,0:T(8,128)S(1)}, f32[8,128]{1,0:T(8,128)S(1)}, u32[]{:S(2)}, u32[]{:S(2)}) %collective-permute-start.8) | collective-permute-done | bytes 4128 | tf_op jit(solution)/shard_map/ppermute | solution.py:278
  39.4 3.0 %collective-permute-start.9 = (f32[8,128]{1,0:T(8,128)S(1)}, f32[8,128]{1,0:T(8,128)S(1)}, u32[]{:S(2)}, u32[]{:S(2)}) collective-permute-start(f32[8,128]{1,0:T(8,128)S(1)} %max.16), channel_id=1, source_target_pairs={{0,5},{1,4},{2,7},{3,6},{4,1},{5,0},{6,3},{7,2},{8,13},{9,12},{10,... | collective-permute-start | bytes 12296 | tf_op jit(solution)/shard_map/ppermute | solution.py:278
  42.4 1.3 %collective-permute-done.9 = f32[8,128]{1,0:T(8,128)S(1)} collective-permute-done((f32[8,128]{1,0:T(8,128)S(1)}, f32[8,128]{1,0:T(8,128)S(1)}, u32[]{:S(2)}, u32[]{:S(2)}) %collective-permute-start.9) | collective-permute-done | bytes 4128 | tf_op jit(solution)/shard_map/ppermute | solution.py:278
  43.7 1.0 %collective-permute-start.10 = (f32[8,128]{1,0:T(8,128)S(1)}, f32[8,128]{1,0:T(8,128)S(1)}, u32[]{:S(2)}, u32[]{:S(2)}) collective-permute-start(f32[8,128]{1,0:T(8,128)S(1)} %max.17), channel_id=1, source_target_pairs={{0,9},{1,8},{2,11},{3,10},{4,13},{5,12},{6,15},{7,14},{8,1},{9,0},... | collective-permute-start | bytes 12296 | tf_op jit(solution)/shard_map/ppermute | solution.py:278
  44.7 2.0 %collective-permute-done.10 = f32[8,128]{1,0:T(8,128)S(1)} collective-permute-done((f32[8,128]{1,0:T(8,128)S(1)}, f32[8,128]{1,0:T(8,128)S(1)}, u32[]{:S(2)}, u32[]{:S(2)}) %collective-permute-start.10) | collective-permute-done | bytes 4128 | tf_op jit(solution)/shard_map/ppermute | solution.py:278
  46.8 1.2 %collective-permute-start.11 = (f32[8,128]{1,0:T(8,128)S(1)}, f32[8,128]{1,0:T(8,128)S(1)}, u32[]{:S(2)}, u32[]{:S(2)}) collective-permute-start(f32[8,128]{1,0:T(8,128)S(1)} %max.18), channel_id=1, source_target_pairs={{0,17},{1,16},{2,19},{3,18},{4,21},{5,20},{6,23},{7,22},{8,25},{9,... | collective-permute-start | bytes 12296 | tf_op jit(solution)/shard_map/ppermute | solution.py:278
  48.0 0.9 %fusion.1 = bf16[64,1024]{1,0:T(8,128)(2,1)} fusion(bf16[64,256]{1,0:T(8,128)(2,1)S(1)} %get-tuple-element.14, bf16[96,1024]{1,0:T(8,128)(2,1)S(1)} %collective-permute-done.6.refs_2_, bf16[32,1024]{1,0:T(8,128)(2,1)S(1)} %collective-permute-done.5, bf16[64,1024]{1,0:T(8,128)(2,1)S(1)} %collective-permute-done.4, bf16[64,1024]{1,0:T(8,128)(2,1)S(1)} %fusion), kind=kOutput, calls=%fused_computation.4 | convolution fusion | flops 35717120 | bytes 688128 | tf_op jit(solution)/shard_map/dot_general | solution.py:254
  48.8 0.6 %copy.8 = f32[5120]{0:T(1024)} copy(f32[5120]{0:T(1024)S(1)} %bitcast.11) | data formatting | bytes 40960
  49.5 0.3 collective-permute-done.11
  49.8 0.5 %slice.19 = f32[1,1]{1,0:T(1,128)} slice(f32[8,128]{1,0:T(8,128)S(1)} %max.19), slice={[0:1], [0:1]} | slice | bytes 8 | tf_op jit(solution)/shard_map/slice | solution.py:316
  (11 shorter events, 0.1 us)
Async XLA Ops:
  0.6 2.9 %copy-start.1 = (s32[32,64]{1,0:T(8,128)S(1)}, s32[32,64]{1,0:T(8,128)}, u32[]{:S(2)}) copy-start(s32[32,64]{1,0:T(8,128)} %picks_ref.3) | copy-start | bytes 24580
  2.9 1.5 %collective-permute-start = (bf16[64,1024]{1,0:T(8,128)(2,1)S(1)}, bf16[64,1024]{1,0:T(8,128)(2,1)S(1)}, u32[]{:S(2)}, u32[]{:S(2)}) collective-permute-start(bf16[64,1024]{1,0:T(8,128)(2,1)S(1)} %gather_rows.1.refs_0_), channel_id=1, source_target_pairs={{0,1},{1,0},{2,3},{3,2},{4,5},{5,4},{6,7},{7,6},{8,9},{9,8},{10,11... | collective-permute-start | bytes 393224 | tf_op jit(solution)/shard_map/ppermute | solution.py:278
  4.7 9.4 %collective-permute-start.1 = (bf16[64,1024]{1,0:T(8,128)(2,1)S(1)}, bf16[64,1024]{1,0:T(8,128)(2,1)S(1)}, u32[]{:S(2)}, u32[]{:S(2)}) collective-permute-start(bf16[64,1024]{1,0:T(8,128)(2,1)S(1)} %fusion.2), channel_id=1, source_target_pairs={{0,6},{1,5},{2,4},{3,7},{4,2},{5,1},{6,0},{7,3},{8,14},{9,13},{10,... | collective-permute-start | bytes 393224 | tf_op jit(solution)/shard_map/ppermute | solution.py:278
  9.7 5.0 %collective-permute-start.2 = (bf16[32,1024]{1,0:T(8,128)(2,1)S(1)}, bf16[32,1024]{1,0:T(8,128)(2,1)S(1)}, u32[]{:S(2)}, u32[]{:S(2)}) collective-permute-start(bf16[32,1024]{1,0:T(8,128)(2,1)S(1)} %slice_select_fusion.1), channel_id=1, source_target_pairs={{0,2},{1,3},{2,0},{3,1},{4,6},{5,7},{6,4},{7,5},{8,10},{9,11},{10,... | collective-permute-start | bytes 196616 | tf_op jit(solution)/shard_map/ppermute | solution.py:278
  14.7 8.2 %collective-permute-start.3 = (bf16[96,1024]{1,0:T(8,128)(2,1)S(1)}, bf16[96,1024]{1,0:T(8,128)(2,1)S(1)}, u32[]{:S(2)}, u32[]{:S(2)}) collective-permute-start(bf16[96,1024]{1,0:T(8,128)(2,1)S(1)} %constant_dynamic-update-slice_fusion.refs_3_), channel_id=1, source_target_pairs={{0,1},{1,0},{2,3},{3,2},{4,5},{5,4},{6,7},{7,6},{8,9},{9,8},{10,11... | collective-permute-start | bytes 589832 | tf_op jit(solution)/shard_map/ppermute | solution.py:278
  14.7 4.0 %copy-start = (bf16[5120,1024]{1,0:T(8,128)(2,1)S(1)}, bf16[5120,1024]{1,0:T(8,128)(2,1)}, u32[]{:S(2)}) copy-start(bf16[5120,1024]{1,0:T(8,128)(2,1)} %points_ref.3) | copy-start | bytes 31457284
  23.1 5.8 %collective-permute-start.4 = (bf16[64,1024]{1,0:T(8,128)(2,1)S(1)}, bf16[64,1024]{1,0:T(8,128)(2,1)S(1)}, u32[]{:S(2)}, u32[]{:S(2)}) collective-permute-start(bf16[64,1024]{1,0:T(8,128)(2,1)S(1)} %fusion), channel_id=1, source_target_pairs={{0,8},{1,25},{2,10},{3,27},{4,12},{5,29},{6,14},{7,31},{8,0},{9,17... | collective-permute-start | bytes 393224 | tf_op jit(solution)/shard_map/ppermute | solution.py:278
  24.8 5.4 %collective-permute-start.5 = (bf16[32,1024]{1,0:T(8,128)(2,1)S(1)}, bf16[32,1024]{1,0:T(8,128)(2,1)S(1)}, u32[]{:S(2)}, u32[]{:S(2)}) collective-permute-start(bf16[32,1024]{1,0:T(8,128)(2,1)S(1)} %slice_select_fusion), channel_id=1, source_target_pairs={{0,16},{1,17},{2,18},{3,19},{4,20},{5,21},{6,22},{7,23},{8,24},{9,... | collective-permute-start | bytes 196616 | tf_op jit(solution)/shard_map/ppermute | solution.py:278
  30.2 3.1 %collective-permute-start.6 = (bf16[96,1024]{1,0:T(8,128)(2,1)S(1)}, bf16[96,1024]{1,0:T(8,128)(2,1)S(1)}, u32[]{:S(2)}, u32[]{:S(2)}) collective-permute-start(bf16[96,1024]{1,0:T(8,128)(2,1)S(1)} %constant_dynamic-update-slice_fusion.2.refs_1_), channel_id=1, source_target_pairs={{0,1},{1,0},{2,3},{3,2},{4,5},{5,4},{6,7},{7,6},{8,9},{9,8},{10,11... | collective-permute-start | bytes 589832 | tf_op jit(solution)/shard_map/ppermute | solution.py:278
  35.1 1.2 %collective-permute-start.7 = (f32[8,128]{1,0:T(8,128)S(1)}, f32[8,128]{1,0:T(8,128)S(1)}, u32[]{:S(2)}, u32[]{:S(2)}) collective-permute-start(f32[8,128]{1,0:T(8,128)S(1)} %get-tuple-element.20), channel_id=1, source_target_pairs={{0,1},{1,0},{2,3},{3,2},{4,5},{5,4},{6,7},{7,6},{8,9},{9,8},{10,11... | collective-permute-start | bytes 12296 | tf_op jit(solution)/shard_map/ppermute | solution.py:278
  36.3 3.0 %collective-permute-start.8 = (f32[8,128]{1,0:T(8,128)S(1)}, f32[8,128]{1,0:T(8,128)S(1)}, u32[]{:S(2)}, u32[]{:S(2)}) collective-permute-start(f32[8,128]{1,0:T(8,128)S(1)} %max.15), channel_id=1, source_target_pairs={{0,3},{1,2},{2,1},{3,0},{4,7},{5,6},{6,5},{7,4},{8,11},{9,10},{10,... | collective-permute-start | bytes 12296 | tf_op jit(solution)/shard_map/ppermute | solution.py:278
  39.4 4.3 %collective-permute-start.9 = (f32[8,128]{1,0:T(8,128)S(1)}, f32[8,128]{1,0:T(8,128)S(1)}, u32[]{:S(2)}, u32[]{:S(2)}) collective-permute-start(f32[8,128]{1,0:T(8,128)S(1)} %max.16), channel_id=1, source_target_pairs={{0,5},{1,4},{2,7},{3,6},{4,1},{5,0},{6,3},{7,2},{8,13},{9,12},{10,... | collective-permute-start | bytes 12296 | tf_op jit(solution)/shard_map/ppermute | solution.py:278
  43.7 3.0 %collective-permute-start.10 = (f32[8,128]{1,0:T(8,128)S(1)}, f32[8,128]{1,0:T(8,128)S(1)}, u32[]{:S(2)}, u32[]{:S(2)}) collective-permute-start(f32[8,128]{1,0:T(8,128)S(1)} %max.17), channel_id=1, source_target_pairs={{0,9},{1,8},{2,11},{3,10},{4,13},{5,12},{6,15},{7,14},{8,1},{9,0},... | collective-permute-start | bytes 12296 | tf_op jit(solution)/shard_map/ppermute | solution.py:278
  46.8 3.0 %collective-permute-start.11 = (f32[8,128]{1,0:T(8,128)S(1)}, f32[8,128]{1,0:T(8,128)S(1)}, u32[]{:S(2)}, u32[]{:S(2)}) collective-permute-start(f32[8,128]{1,0:T(8,128)S(1)} %max.18), channel_id=1, source_target_pairs={{0,17},{1,16},{2,19},{3,18},{4,21},{5,20},{6,23},{7,22},{8,25},{9,... | collective-permute-start | bytes 12296 | tf_op jit(solution)/shard_map/ppermute | solution.py:278
